TPU v7x, 32 devices: a whole 2x2x4 slice. The times are simulated.
32 devices in a mesh: gx: 4 (over z), gy: 8 (over y, x, core).
Axes of the slice: x: 2, y: 2, z: 4, core: 2. Of those that a mesh axis runs over, the one named last changes fastest.
Arguments:
- matrix_rows: float32 [4096, 1024], P(('gx', 'gy')), may hold values from -1.1 to 1.1
- tile_owner: int32 [136], replicated, may hold values from 0 to 31, as said below
- tile_slot: int32 [136], replicated, may hold values from 0 to 4, as said below
Outputs:
- packed_tiles: float32 [160, 256, 256], P(('gx', 'gy'))
Inputs may be any that keep to these rules, and one draw needn't show every extreme that they name: `tile_owner`: give tile (I, J) the class (c, r) as follows, with a = I // 4, b = J // 4, i = I % 4, j = J % 4: if a == b, c = a and r = i when i - j < 2, else r = j; if a > b and (a - b > 2, or a - b == 2 with i + j even), c = b and r = i; otherwise c = a and r = j. The owner of a class (c, r) tile is one of the devices c * 8 to c * 8 + 7. Every owner holds 4 or 5 tiles. At most 2 tiles of one class share an owner, and in every draw some owner holds exactly 2 tiles of one class. `tile_slot`: the tiles of one owner take the slots 0 to their count - 1, each once.
All inputs are finite; a program needn't handle non-finite values.
Results may differ from a plain program's by a relative error of at most 0.0003.
Values sent between devices are 32-bit elements; how exact they have to be, the bound alone decides.
A program may use at most 128 MiB of HBM per device.

v0:
```python
import functools

import jax
import jax.numpy as jnp
from jax import lax
from jax.experimental import pallas as pl
from jax.experimental.pallas import tpu as pltpu
from jax.sharding import PartitionSpec as P

MESH = pl.DeviceIdType.MESH


def chip_position(chip, chips):
    row, col = lax.div(chip, 2), lax.rem(chip, 2)
    return col * (1 + row) + (1 - col) * lax.rem(chips - row, chips)


def chip_at(position, chips):
    behind = lax.rem(position + chips - 1, chips)
    far = lax.div(behind, chips // 2)
    return (1 - far) * (2 * behind + 1) + far * 2 * (chips - 1 - behind)


def piece_lists(half_tiles, half_x):
    lists, start = [], 0
    for step in range(half_x + 1):
        if step == 0:
            count = half_tiles // 2 + 1
        elif step < half_x:
            count = half_tiles
        else:
            count = half_tiles // 2
        lists.append((step, start, count))
        start += count
    return lists, start


def piece(x, r, step, i, nx, half_tiles, half_x):
    source = lax.rem(x - step + nx, nx)
    if step == 0:
        col = lax.rem(r - i + half_tiles, half_tiles)
        valid = jnp.logical_or(i < half_tiles // 2, r < half_tiles // 2)
        rowwise = col <= r
    elif step < half_x:
        col = i
        valid = i >= 0
        rowwise = source > x
    else:
        flag = jnp.where(x >= half_x, 1, 0)
        col = 2 * i + lax.rem(r + flag, 2)
        valid = i >= 0
        rowwise = source > x
    other, mine = source * half_tiles + r, x * half_tiles + col
    row_tile = jnp.where(rowwise, other, mine)
    col_tile = jnp.where(rowwise, mine, other)
    tile = jnp.where(valid, row_tile * (row_tile + 1) // 2 + col_tile, 0)
    return col, valid, rowwise, tile


def kernel(
    dims, rows_ref, owner_ref, slot_ref, out_ref,
    gath, zbuf, chi, clo, zsplit, pieces, outgoing, incoming, targets,
    gs_r, gr_r, gs_l, gr_l, ss, sr, zs, zr, xs, xr,
):
    nx, ny, half_tiles, half_x, capacity, slots = dims
    rows = rows_ref.shape[0]
    half = rows // 2
    chips = ny // 2
    reach = chips // 2
    x = lax.axis_index("gx")
    y = lax.axis_index("gy")
    core = lax.rem(y, 2)
    chip = lax.div(y, 2)
    right_x, left_x = lax.rem(x + 1, nx), lax.rem(x + nx - 1, nx)
    sibling = y + 1 - 2 * core
    place = chip_position(chip, chips)

    def at(position):
        return 2 * chip_at(lax.rem(position + chips, chips), chips) + core

    next_y, prev_y = at(place + 1), at(place - 1)
    lists, piece_count = piece_lists(half_tiles, half_x)

    barrier = pltpu.get_barrier_semaphore()
    for other in (right_x, left_x):
        pl.semaphore_signal(barrier, inc=1, device_id=(other, y), device_id_type=MESH)
    for offset in range(1, ny):
        pl.semaphore_signal(
            barrier, inc=1, device_id=(x, lax.rem(y + offset, ny)), device_id_type=MESH
        )
    pl.semaphore_wait(barrier, ny + 1)

    started = []

    def send(src, dst, send_sem, recv_sem, target):
        copy = pltpu.make_async_remote_copy(
            src_ref=src, dst_ref=dst, send_sem=send_sem, recv_sem=recv_sem,
            device_id=target, device_id_type=MESH,
        )
        copy.start()
        started.append(copy)

    def part(h):
        return pl.ds(h * half, half)

    def zcopy(step, h):
        src = rows_ref.at[part(h)] if step == 1 else zbuf.at[step - 2, part(h)]
        send(src, zbuf.at[step - 1, part(h)], zs.at[step - 1, h], zr.at[step - 1, h], (right_x, y))

    def block(owner, h):
        return gath.at[owner, part(h)]

    def ring(direction, distance, h):
        owner = at(place - direction * (distance - 1))
        src = rows_ref.at[part(h)] if distance == 1 else block(owner, h)
        s, r = (gs_r, gr_r) if direction == 1 else (gs_l, gr_l)
        target = next_y if direction == 1 else prev_y
        send(src, block(owner, h), s.at[distance - 1, h], r.at[distance - 1, h], (x, target))

    def cross(number, owner, h):
        src = rows_ref.at[part(h)] if number == 0 else block(owner, h)
        send(src, block(owner, h), ss.at[number, h], sr.at[number, h], (x, sibling))

    def halves_of(direction, distance):
        if distance < reach:
            return (0, 1) if direction == 1 else (1, 0)
        return (0,) if direction == 1 else (1,)

    def split(value, hi_ref, lo_ref, index):
        hi = value.astype(jnp.bfloat16)
        hi_ref[index] = hi
        lo_ref[index] = (value - hi.astype(jnp.float32)).astype(jnp.bfloat16)

    zcopy(1, 0)
    ring(1, 1, 0)
    if reach > 1:
        ring(-1, 1, 1)
        zcopy(1, 1)
        ring(1, 1, 1)
        ring(-1, 1, 0)
    else:
        ring(-1, 1, 1)
        zcopy(1, 1)
    cross(0, y, 0)
    cross(0, y, 1)

    for step, first, count in lists:
        def fill(i, carry, step=step, first=first):
            _, valid, _, tile = piece(x, chip, step, i, nx, half_tiles, half_x)
            targets[first + i] = jnp.where(valid, lax.rem(owner_ref[tile], ny), ny)
            return carry
        lax.fori_loop(0, count, fill, 0)

    me = x * ny + y

    def class_loop(r, carry):
        state = (jnp.int32(0),) + carry
        for step, first, count in lists:
            def look(i, state, step=step):
                seen, found = state[0], state[1:]
                _, valid, rowwise, tile = piece(x, r, step, i, nx, half_tiles, half_x)
                mine = jnp.where(valid, jnp.where(owner_ref[tile] == me, 1, 0), 0)
                slot = slot_ref[tile]
                code = 2 * (r * capacity + jnp.minimum(seen, capacity - 1))
                code = code + jnp.where(rowwise, 1, 0)
                key = jnp.where(mine == 1, slot, slots)
                found = tuple(jnp.where(key == s, code, found[s]) for s in range(slots))
                return (seen + mine,) + found
            state = lax.fori_loop(0, count, look, state)
        return state[1:]

    found = lax.fori_loop(0, half_tiles, class_loop, (jnp.int32(-1),) * slots)

    chosen = []
    for offset in range(ny):
        dest = lax.rem(y + offset, ny)

        def pick(p, state, dest=dest):
            hit = jnp.where(targets[p] == dest, 1, 0)
            seen = state[0]
            key = jnp.where(hit == 1, seen, capacity)
            picks = tuple(jnp.where(key == k, p, state[1 + k]) for k in range(capacity))
            return (seen + hit,) + picks

        chosen.append(lax.fori_loop(0, piece_count, pick, (jnp.int32(0),) * (capacity + 1))[1:])

    def wait_recv(dst, sem):
        pltpu.make_async_remote_copy(
            src_ref=dst, dst_ref=dst, send_sem=sem, recv_sem=sem,
            device_id=(x, sibling), device_id_type=MESH,
        ).wait_recv()

    def split_other(step, h):
        ref = rows_ref.at[part(h)] if step == 0 else zbuf.at[step - 1, part(h)]
        value = ref[...]
        hi = value.astype(jnp.bfloat16)
        zsplit[step, h, :half] = hi
        zsplit[step, h, half:] = (value - hi.astype(jnp.float32)).astype(jnp.bfloat16)

    def take_other(step, h):
        wait_recv(zbuf.at[step - 1, part(h)], zr.at[step - 1, h])
        if step < half_x:
            zcopy(step + 1, h)

    split_other(0, 0)
    split_other(0, 1)
    split(rows_ref[...], chi, clo, y)

    def take_cross(number, owner, halves):
        for h in halves:
            wait_recv(block(owner, h), sr.at[number, h])

    one = functools.partial(
        lax.dot_general,
        dimension_numbers=(((1,), (1,)), ((), ())),
        preferred_element_type=jnp.float32,
    )
    width = rows_ref.shape[1]
    row_inside = core * rows + lax.broadcasted_iota(jnp.int32, (half, 2 * rows), 0)
    col_inside = lax.broadcasted_iota(jnp.int32, (half, 2 * rows), 1)

    def one_piece_of(h):
        above = jnp.where(row_inside + h * half < col_inside, 1, 0)

        def one_piece(i, step, first, col):
            b_hi = chi[pl.ds(2 * col, 2)].reshape(2 * rows, width)
            b_lo = clo[pl.ds(2 * col, 2)].reshape(2 * rows, width)
            both = one(zsplit[step, h], b_hi)
            full = both[:half] + (both[half:] + one(zsplit[step, h, :half], b_lo))
            if step == 0:
                full = jnp.where(above * jnp.where(i == 0, 1, 0) == 1, 0.0, full)
            pieces[h, first + i, 0] = full[:, :rows]
            pieces[h, first + i, 1] = full[:, rows:]

        return one_piece

    farthest = chip_at(lax.rem(place + reach, chips), chips)
    soon = min(reach, half_x) if reach > 1 else 0

    def multiply(h, mode):
        one_piece = one_piece_of(h)
        for step, first, count in lists:
            if mode == "early" and step >= soon:
                continue

            def make(i, carry, step=step, first=first):
                col, _, _, _ = piece(x, chip, step, i, nx, half_tiles, half_x)
                if mode == "all" or step >= soon:
                    one_piece(i, step, first, col)
                else:
                    wanted = (col != farthest) if mode == "early" else (col == farthest)
                    pl.when(wanted)(lambda: one_piece(i, step, first, col))
                return carry
            lax.fori_loop(0, count, make, 0)

    pending = [(0, sibling, (0, 1))]
    for distance in range(1, reach + 1):
        if distance == reach:
            for number, owner, halves in pending[1:]:
                take_cross(number, owner, halves)
                split(gath[owner], chi, clo, owner)
            multiply(0, "early")
        if distance <= half_x:
            for h in (0, 1):
                if (distance, h) != (half_x, 1):
                    take_other(distance, h)
                if h in halves_of(1, distance):
                    owner = at(place - distance)
                    wait_recv(block(owner, h), gr_r.at[distance - 1, h])
                    if distance < reach and h in halves_of(1, distance + 1):
                        ring(1, distance + 1, h)
                    cross(2 * distance - 1, owner, h)
                g = 1 - h
                if g in halves_of(-1, distance):
                    owner = at(place + distance)
                    wait_recv(block(owner, g), gr_l.at[distance - 1, g])
                    if distance < reach and g in halves_of(-1, distance + 1):
                        ring(-1, distance + 1, g)
                    cross(2 * distance, owner, g)
            split_other(distance, 0)
            if distance < half_x:
                split_other(distance, 1)
        behind, ahead = at(place - distance), at(place + distance)
        pending.append((2 * distance - 1, behind + 1 - 2 * core, halves_of(1, distance)))
        pending.append((2 * distance, ahead + 1 - 2 * core, halves_of(-1, distance)))
        split(gath[behind], chi, clo, behind)
        if distance < reach:
            split(gath[ahead], chi, clo, ahead)
        for number, owner, halves in pending[: (1 if distance == 1 else 0)]:
            take_cross(number, owner, halves)
            split(gath[owner], chi, clo, owner)
    for number, owner, halves in pending[-2:]:
        take_cross(number, owner, halves)
    split(gath[pending[-1][1]], chi, clo, pending[-1][1])
    for step in range(reach + 1, half_x + 1):
        for h in (0, 1):
            if (step, h) != (half_x, 1):
                take_other(step, h)
                split_other(step, h)

    def arrival(offset):
        return pl.ds(offset * capacity * 2, capacity * 2)

    def exchange(h, offset):
        send(
            outgoing.at[h, offset], incoming.at[h, arrival(offset)],
            xs.at[h, offset], xr.at[h, offset], (x, lax.rem(y + offset, ny)),
        )

    for h in (0, 1):
        if h == 1:
            take_other(half_x, 1)
            split_other(half_x, 1)
        multiply(h, "all" if h == 1 else "late")
        for offset in range(1, ny):
            for k in range(capacity):
                outgoing[h, offset, 2 * k:2 * k + 2] = pieces[h, chosen[offset][k]]
            if offset > 1:
                exchange(h, offset - 1)
        for k in range(capacity):
            incoming[h, 2 * k:2 * k + 2] = pieces[h, chosen[0][k]]
        exchange(h, ny - 1)
    for h in (0, 1):
        for offset in range(1, ny):
            wait_recv(incoming.at[h, arrival(offset)], xr.at[h, offset])

    for s in range(slots):
        code = found[s]
        there = code >= 0
        safe = jnp.maximum(code, 0)
        rowwise = lax.rem(safe, 2) == 1
        rank = lax.rem(safe // 2, capacity)
        first_source = 2 * (safe // (2 * capacity))
        bases = [
            (lax.rem(y - first_source - h + ny, ny) * capacity + rank) * 2 for h in (0, 1)
        ]
        for i in (0, 1):
            for j in (0, 1):
                place_of = jnp.where(rowwise, bases[i] + j, bases[j] + i)
                value = jnp.concatenate([incoming[0, place_of], incoming[1, place_of]], axis=0)
                value = jnp.where(rowwise, value, value.T)
                out_ref[s, i * rows:(i + 1) * rows, j * rows:(j + 1) * rows] = jnp.where(
                    there, value, 0.0
                )
    for copy in started:
        copy.wait_send()


def per_device(mesh_shape, matrix_rows, tile_owner, tile_slot):
    nx, ny = mesh_shape
    rows, width = matrix_rows.shape
    half_tiles, half_x = ny // 2, nx // 2
    capacity = nx // 4 + 1
    slots = -(-tile_owner.shape[0] // (nx * ny))
    _, piece_count = piece_lists(half_tiles, half_x)
    reach = max(ny // 4, 1)
    f32, bf16 = jnp.float32, jnp.bfloat16
    dma = pltpu.SemaphoreType.DMA
    return pl.pallas_call(
        functools.partial(kernel, (nx, ny, half_tiles, half_x, capacity, slots)),
        out_shape=jax.ShapeDtypeStruct((slots, 2 * rows, 2 * rows), f32),
        in_specs=[
            pl.BlockSpec(memory_space=pltpu.VMEM),
            pl.BlockSpec(memory_space=pltpu.SMEM),
            pl.BlockSpec(memory_space=pltpu.SMEM),
        ],
        out_specs=pl.BlockSpec(memory_space=pltpu.VMEM),
        scratch_shapes=[
            pltpu.VMEM((ny, rows, width), f32),
            pltpu.VMEM((half_x, rows, width), f32),
            pltpu.VMEM((ny, rows, width), bf16),
            pltpu.VMEM((ny, rows, width), bf16),
            pltpu.VMEM((half_x + 1, 2, rows, width), bf16),
            pltpu.VMEM((2, piece_count, 2, rows // 2, rows), f32),
            pltpu.VMEM((2, ny, 2 * capacity, rows // 2, rows), f32),
            pltpu.VMEM((2, ny * 2 * capacity, rows // 2, rows), f32),
            pltpu.SMEM((piece_count,), jnp.int32),
            dma((reach, 2)), dma((reach, 2)), dma((reach, 2)), dma((reach, 2)),
            dma((2 * reach + 1, 2)), dma((2 * reach + 1, 2)),
            dma((half_x, 2)), dma((half_x, 2)),
            dma((2, ny)), dma((2, ny)),
        ],
        compiler_params=pltpu.CompilerParams(
            collective_id=0, has_side_effects=True, vmem_limit_bytes=60 * 1024 * 1024
        ),
    )(matrix_rows, tile_owner, tile_slot)


def solution(mesh):
    placed = (P(("gx", "gy"), None), P(), P())
    return jax.shard_map(
        functools.partial(per_device, (mesh.shape["gx"], mesh.shape["gy"])),
        mesh=mesh,
        in_specs=placed,
        out_specs=P(("gx", "gy"), None, None),
        check_vma=False,
    )
```

profile of v0, /device:TPU:1, one launch (start us, length us, event | category | flops | bytes accessed | tf_op | source)
XLA Modules:
  0.0 57.8 jit_solution(13847068349267072085)
XLA Ops:
  0.0 55.3 %shard_map.37 = f32[5,256,256]{2,1,0:T(8,128)} custom-call(f32[128,1024]{1,0:T(8,128)} %rows_ref.1, s32[136]{0:T(256)} %owner_ref.1, s32[136]{0:T(256)} %slot_ref.1), custom_call_target="tpu_custom_call" | custom-call | tf_op jit(solution)/shard_map/pallas_call | solution.py:359
  55.3 2.5 %copy.5 = f32[5,256,256]{2,1,0:T(8,128)} copy(f32[5,256,256]{2,1,0:T(8,128)} %shard_map.37) | data formatting | bytes 2621440
where the time goes:
time: 58 us; the launch traced here: 57.8 us
  Pallas kernels  55.3 us (95%)
  local copies, waits for them, and re-layouts  2.51 us (4%)
    pallas_call x1, Pallas kernels, per_device(): pl.pallas_call(functools.partial(kernel, (nx, ny, half_tiles, half_x, cap...  55.3 us
    unnamed x1, local copies, waits for them, and re-layouts  2.51 us

commit v1 on v0

--- a/solution.py
+++ b/solution.py
@@ -346,6 +346,12 @@
         copy.wait_send()
 
 
+def copy_out(in_ref, out_ref, sem):
+    copy = pltpu.make_async_copy(in_ref, out_ref, sem)
+    copy.start()
+    copy.wait()
+
+
 def per_device(mesh_shape, matrix_rows, tile_owner, tile_slot):
     nx, ny = mesh_shape
     rows, width = matrix_rows.shape
@@ -356,7 +362,7 @@
     reach = max(ny // 4, 1)
     f32, bf16 = jnp.float32, jnp.bfloat16
     dma = pltpu.SemaphoreType.DMA
-    return pl.pallas_call(
+    packed = pl.pallas_call(
         functools.partial(kernel, (nx, ny, half_tiles, half_x, capacity, slots)),
         out_shape=jax.ShapeDtypeStruct((slots, 2 * rows, 2 * rows), f32),
         in_specs=[
@@ -381,9 +387,17 @@
             dma((2, ny)), dma((2, ny)),
         ],
         compiler_params=pltpu.CompilerParams(
-            collective_id=0, has_side_effects=True, vmem_limit_bytes=60 * 1024 * 1024
+            collective_id=0, has_side_effects=True, vmem_limit_bytes=44 * 1024 * 1024
         ),
     )(matrix_rows, tile_owner, tile_slot)
+    return pl.pallas_call(
+        copy_out,
+        out_shape=jax.ShapeDtypeStruct(packed.shape, packed.dtype),
+        in_specs=[pl.BlockSpec(memory_space=pltpu.VMEM)],
+        out_specs=pl.BlockSpec(memory_space=pl.ANY),
+        scratch_shapes=[pltpu.SemaphoreType.DMA(())],
+        compiler_params=pltpu.CompilerParams(vmem_limit_bytes=4 * 1024 * 1024),
+    )(packed)
 
 
 def solution(mesh):

time: 58 us -> 57.4 us (0.990)
    pallas_call x1, Pallas kernels: 55.3 us -> 53.7 us  [per_device(): pl.pallas_call(functools.partial(kernel, (nx, ny, half_tiles, half_x, cap...]
    pallas_call x0 -> x1, Pallas kernels: none -> 1.07 us  [per_device(): pl.pallas_call(copy_out, out_shape=jax.ShapeDtypeStruct(packed.shape, pac...]
    unnamed x1 -> x6, local copies, waits for them, and re-layouts: 2.51 us -> 2.4 us
where the time goes in v1:
time: 57.4 us; the launch traced here: 57.2 us
  Pallas kernels  54.8 us (95%)
  local copies, waits for them, and re-layouts  2.4 us (4%)
    pallas_call x1, Pallas kernels, per_device(): pl.pallas_call(functools.partial(kernel, (nx, ny, half_tiles, half_x, cap...  53.7 us
    unnamed x6, local copies, waits for them, and re-layouts  2.4 us

profile of v1, /device:TPU:1, one launch (start us, length us, event | category | flops | bytes accessed | tf_op | source)
XLA Modules:
  0.0 57.2 jit_solution(7597286027512838250)
XLA Ops:
  0.0 0.0 copy-start
  0.0 1.0 %copy-done = f32[128,1024]{1,0:T(8,128)S(1)} copy-done((f32[128,1024]{1,0:T(8,128)S(1)}, f32[128,1024]{1,0:T(8,128)}, u32[]{:S(2)}) %copy-start) | copy-done | bytes 524312
  1.0 0.0 copy-start.1
  1.0 0.7 %copy-done.1 = s32[136]{0:T(256)S(1)} copy-done((s32[136]{0:T(256)S(1)}, s32[136]{0:T(256)}, u32[]{:S(2)}) %copy-start.1) | copy-done | bytes 568
  1.7 0.0 copy-start.2
  1.7 0.7 %copy-done.2 = s32[136]{0:T(256)S(1)} copy-done((s32[136]{0:T(256)S(1)}, s32[136]{0:T(256)}, u32[]{:S(2)}) %copy-start.2) | copy-done | bytes 568
  2.4 53.7 %shard_map.37.in_ref = f32[5,256,256]{2,1,0:T(8,128)S(1)} custom-call(f32[128,1024]{1,0:T(8,128)S(1)} %copy-done, s32[136]{0:T(256)S(1)} %copy-done.1, s32[136]{0:T(256)S(1)} %copy-done.2), custom_call_target="tpu_custom_call" | custom-call | tf_op jit(solution)/shard_map/pallas_call | solution.py:365
  56.1 1.1 %shard_map.38 = f32[5,256,256]{2,1,0:T(8,128)} custom-call(f32[5,256,256]{2,1,0:T(8,128)S(1)} %shard_map.37.in_ref), custom_call_target="tpu_custom_call" | custom-call | tf_op jit(solution)/shard_map/pallas_call | solution.py:393
Async XLA Ops:
  0.0 1.0 %copy-start = (f32[128,1024]{1,0:T(8,128)S(1)}, f32[128,1024]{1,0:T(8,128)}, u32[]{:S(2)}) copy-start(f32[128,1024]{1,0:T(8,128)} %rows_ref.1) | copy-start | bytes 1572868
  1.0 0.7 %copy-start.1 = (s32[136]{0:T(256)S(1)}, s32[136]{0:T(256)}, u32[]{:S(2)}) copy-start(s32[136]{0:T(256)} %owner_ref.1) | copy-start | bytes 1636
  1.7 0.7 %copy-start.2 = (s32[136]{0:T(256)S(1)}, s32[136]{0:T(256)}, u32[]{:S(2)}) copy-start(s32[136]{0:T(256)} %slot_ref.1) | copy-start | bytes 1636

commit v2 on v1

--- a/solution.py
+++ b/solution.py
@@ -346,13 +346,338 @@
         copy.wait_send()
 
 
+def plane_kernel(
+    dims, rows_hbm, owner_hbm, slot_hbm, out_ref,
+    gath, zfar, parts, far_parts, far, extra, owner_ref, slot_ref, todo,
+    ins, ss, rs,
+):
+    nx, ny, half_tiles, slots = dims
+    rows, width = zfar.shape
+    half = rows // 2
+    x = lax.axis_index("gx")
+    y = lax.axis_index("gy")
+    core = lax.rem(y, 2)
+    chip = lax.div(y, 2)
+    twin = 1 - core
+    right, left = (lax.rem(x + 1, nx), y), (lax.rem(x + nx - 1, nx), y)
+    sibling = (x, y + 1 - 2 * core)
+    across = (x, y + 2 - 4 * lax.rem(chip, 2))
+    along = (x, lax.rem(y + 4, ny))
+
+    barrier = pltpu.get_barrier_semaphore()
+    peers = (sibling, across, along, right, left)
+    for other in peers:
+        pl.semaphore_signal(barrier, inc=1, device_id=other, device_id_type=MESH)
+    loads = [
+        pltpu.make_async_copy(rows_hbm, gath.at[0, core], ins.at[0]),
+        pltpu.make_async_copy(owner_hbm, owner_ref, ins.at[1]),
+        pltpu.make_async_copy(slot_hbm, slot_ref, ins.at[2]),
+    ]
+    for copy in loads:
+        copy.start()
+    pl.semaphore_wait(barrier, len(peers))
+    loads[0].wait()
+
+    started, numbers = [], {}
+
+    def number(name):
+        return numbers.setdefault(name, len(numbers))
+
+    def send(name, src, dst, target):
+        i = number(name)
+        copy = pltpu.make_async_remote_copy(
+            src_ref=src, dst_ref=dst, send_sem=ss.at[i], recv_sem=rs.at[i],
+            device_id=target, device_id_type=MESH,
+        )
+        copy.start()
+        started.append(copy)
+
+    def got(name, dst):
+        i = number(name)
+        pltpu.make_async_remote_copy(
+            src_ref=dst, dst_ref=dst, send_sem=rs.at[i], recv_sem=rs.at[i],
+            device_id=sibling, device_id_type=MESH,
+        ).wait_recv()
+
+    def block(where, side, h):
+        return gath.at[where, side, pl.ds(h * half, half)]
+
+    def cross(where, h):
+        send(("cross", where, h), block(where, core, h), block(where, core, h), sibling)
+
+    def crossed(where, h):
+        got(("cross", where, h), block(where, twin, h))
+        split(where, twin, h)
+
+    def split(where, side, h):
+        value = gath[where, side, h * half:(h + 1) * half]
+        hi = value.astype(jnp.bfloat16)
+        parts[where, 0, side, h * half:(h + 1) * half] = hi
+        parts[where, 1, side, h * half:(h + 1) * half] = (
+            value - hi.astype(jnp.float32)
+        ).astype(jnp.bfloat16)
+
+    for h in (0, 1):
+        send(("z", 0, h), block(0, core, h), block(4, core, h), right)
+        send(("x", 0, h), block(0, core, h), block(1, core, h), across)
+        send(("y", 0, 1 - h), block(0, core, 1 - h), block(2, core, 1 - h), along)
+    for h in (0, 1):
+        cross(0, h)
+    for h in (0, 1):
+        split(0, core, h)
+    for copy in loads[1:]:
+        copy.wait()
+
+    me = x * ny + y
+
+    def look(tile, state):
+        i_tile, j_tile = state[0], state[1]
+        a, i = lax.div(i_tile, half_tiles), lax.rem(i_tile, half_tiles)
+        b, j = lax.div(j_tile, half_tiles), lax.rem(j_tile, half_tiles)
+        i_chip, j_chip = jnp.bitwise_xor(i, chip), jnp.bitwise_xor(j, chip)
+        i_near, j_near = jnp.where(a == x, 0, half_tiles), jnp.where(b == x, 0, half_tiles)
+        same = jnp.where(i_tile == j_tile, 256, 0)
+        last = jnp.where((i_near + i_chip == 7) | (j_near + j_chip == 7), 64, 0)
+        near = i_near + i_chip + 8 * (j_near + j_chip) + same + last
+        far_code = 128 + jnp.where(
+            a == x, j_chip + 8 * lax.div(i, 2), i_chip + 8 * lax.div(j, 2)
+        )
+        code = jnp.where(a - b == nx // 2, far_code, near)
+        key = jnp.where(owner_ref[tile] == me, slot_ref[tile], slots)
+        found = tuple(jnp.where(key == s, code, state[2 + s]) for s in range(slots))
+        wrap = j_tile == i_tile
+        return (
+            jnp.where(wrap, i_tile + 1, i_tile), jnp.where(wrap, 0, j_tile + 1)
+        ) + found
+
+    codes = lax.fori_loop(
+        0, owner_ref.shape[0], look, (jnp.int32(0),) * 2 + (jnp.int32(-1),) * slots
+    )[2:]
+    seen, picks, ranks = jnp.int32(0), [jnp.int32(0)] * 2, []
+    kinds = []
+    for s in range(slots):
+        code = codes[s]
+        kind = jnp.where(code < 0, 3, lax.rem(lax.div(code, 64), 4))
+        kinds.append(kind)
+        todo[s] = jnp.where(kind == 0, code, 0)
+        is_last = jnp.where(kind == 1, 1, 0)
+        ranks.append(seen)
+        picks = [
+            jnp.where(is_last * jnp.where(seen == k, 1, 0) == 1, code, picks[k])
+            for k in range(2)
+        ]
+        seen = seen + is_last
+    for k in range(2):
+        todo[slots + k] = picks[k]
+
+    one = functools.partial(
+        lax.dot_general,
+        dimension_numbers=(((1,), (1,)), ((), ())),
+        preferred_element_type=jnp.float32,
+    )
+
+    def product(code):
+        first, second = lax.rem(code, 8), lax.rem(lax.div(code, 8), 8)
+        both = one(
+            parts[first].reshape(4 * rows, width), parts[second, 0].reshape(2 * rows, width)
+        )
+        return both[:2 * rows] + (
+            both[2 * rows:]
+            + one(
+                parts[first, 0].reshape(2 * rows, width),
+                parts[second, 1].reshape(2 * rows, width),
+            )
+        )
+
+    got(("x", 0, 0), block(1, core, 0))
+    send(("y", 3, 0), block(1, core, 0), block(3, core, 0), along)
+    got(("y", 0, 1), block(2, core, 1))
+    send(("x", 3, 1), block(2, core, 1), block(3, core, 1), across)
+    cross(1, 0)
+    cross(2, 1)
+    got(("z", 0, 0), block(4, core, 0))
+    send(("z", 1, 0), block(4, core, 0), zfar.at[pl.ds(0, half)], right)
+    cross(4, 0)
+    split(1, core, 0)
+    split(2, core, 1)
+    split(4, core, 0)
+    crossed(0, 0)
+    crossed(0, 1)
+    crossed(1, 0)
+    crossed(2, 1)
+    crossed(4, 0)
+    got(("x", 0, 1), block(1, core, 1))
+    cross(1, 1)
+    got(("y", 0, 0), block(2, core, 0))
+    cross(2, 0)
+    got(("z", 0, 1), block(4, core, 1))
+    send(("z", 1, 1), block(4, core, 1), zfar.at[pl.ds(half, half)], right)
+    for h in (0, 1):
+        send(("x", 4, h), block(4, core, h), block(5, core, h), across)
+        send(("y", 4, h), block(4, core, h), block(6, core, h), along)
+    cross(4, 1)
+    split(1, core, 1)
+    split(2, core, 0)
+    split(4, core, 1)
+    crossed(1, 1)
+    crossed(2, 0)
+    crossed(4, 1)
+    got(("y", 3, 0), block(3, core, 0))
+    cross(3, 0)
+    got(("x", 3, 1), block(3, core, 1))
+    cross(3, 1)
+    for h in (0, 1):
+        send(("z", 3, h), block(3, core, h), block(7, core, h), right)
+    split(3, core, 0)
+    split(3, core, 1)
+    crossed(3, 0)
+    crossed(3, 1)
+
+    def split_far(h):
+        part = slice(h * half, (h + 1) * half)
+        value = zfar[part]
+        hi = value.astype(jnp.bfloat16)
+        far_parts[0, part] = hi
+        far_parts[1, part] = (value - hi.astype(jnp.float32)).astype(jnp.bfloat16)
+
+    flag = jnp.where(x >= nx // 2, 1, 0)
+    got(("z", 1, 0), zfar.at[pl.ds(0, half)])
+    split_far(0)
+    got(("z", 1, 1), zfar.at[pl.ds(half, half)])
+    split_far(1)
+    for t in (0, 1):
+        col = flag + 2 * lax.rem(t + lax.div(chip, 2), 2)
+        both = one(
+            far_parts[...].reshape(2 * rows, width), parts[col, 0].reshape(2 * rows, width)
+        )
+        full = both[:rows] + (
+            both[rows:] + one(far_parts[0], parts[col, 1].reshape(2 * rows, width))
+        )
+        for k in (0, 1):
+            piece_k = full[:, k * rows:(k + 1) * rows]
+            far[0, core, t, k] = jnp.where(flag == 0, piece_k, piece_k.T)
+
+    def far_at(where, side, t):
+        return far.at[where, side, t]
+
+    def far_cross(where, t):
+        send(("fcross", where, t), far_at(where, core, t), far_at(where, core, t), sibling)
+
+    for t in (0, 1):
+        send(("fx", 0, t), far_at(0, core, t), far_at(1, core, t), across)
+        send(("fy", 0, 1 - t), far_at(0, core, 1 - t), far_at(2, core, 1 - t), along)
+    for t in (0, 1):
+        far_cross(0, t)
+
+    for h in (0, 1):
+        got(("x", 4, h), block(5, core, h))
+        cross(5, h)
+        got(("y", 4, h), block(6, core, h))
+        cross(6, h)
+        split(5, core, h)
+        split(6, core, h)
+        crossed(5, h)
+        crossed(6, h)
+
+    above = jnp.where(
+        lax.broadcasted_iota(jnp.int32, (2 * rows, 2 * rows), 0)
+        < lax.broadcasted_iota(jnp.int32, (2 * rows, 2 * rows), 1), 1, 0,
+    )
+
+    def local(s, carry):
+        code = todo[s]
+        masked = jnp.where(code >= 256, 1, 0)
+        out_ref[s] = jnp.where(above * masked == 1, 0.0, product(code))
+        return carry
+
+    middle = slots // 2
+    lax.fori_loop(0, middle, local, 0)
+    got(("fx", 0, 0), far_at(1, core, 0))
+    send(("fy", 3, 0), far_at(1, core, 0), far_at(3, core, 0), along)
+    got(("fy", 0, 1), far_at(2, core, 1))
+    send(("fx", 3, 1), far_at(2, core, 1), far_at(3, core, 1), across)
+    far_cross(1, 0)
+    far_cross(2, 1)
+    got(("z", 3, 0), block(7, core, 0))
+    cross(7, 0)
+    lax.fori_loop(middle, slots, local, 0)
+    split(7, core, 0)
+    crossed(7, 0)
+    got(("fx", 0, 1), far_at(1, core, 1))
+    far_cross(1, 1)
+    got(("fy", 0, 0), far_at(2, core, 0))
+    far_cross(2, 0)
+    got(("z", 3, 1), block(7, core, 1))
+    cross(7, 1)
+    split(7, core, 1)
+    crossed(7, 1)
+
+    def behind(k, carry):
+        extra[k] = product(todo[slots + k])
+        return carry
+
+    lax.fori_loop(0, 2, behind, 0)
+    got(("fy", 3, 0), far_at(3, core, 0))
+    far_cross(3, 0)
+    got(("fx", 3, 1), far_at(3, core, 1))
+    far_cross(3, 1)
+    for where in range(4):
+        for t in (0, 1):
+            got(("fcross", where, t), far_at(where, twin, t))
+
+    for s in range(slots):
+        kind, code = kinds[s], jnp.maximum(codes[s], 0)
+        where = lax.rem(code, 4)
+        t = lax.rem(lax.div(code, 8), 2)
+        rank = jnp.minimum(ranks[s], 1)
+        for i in (0, 1):
+            for j in (0, 1):
+                side, k = jnp.where(flag == 0, i, j), jnp.where(flag == 0, j, i)
+                at = (s, slice(i * rows, (i + 1) * rows), slice(j * rows, (j + 1) * rows))
+                value = jnp.where(kind == 1, extra[rank, at[1], at[2]], out_ref[at])
+                value = jnp.where(kind == 2, far[where, side, t, k], value)
+                out_ref[at] = jnp.where(kind == 3, 0.0, value)
+    for copy in started:
+        copy.wait_send()
+
+
+def plane_call(dims, matrix_rows, tile_owner, tile_slot):
+    nx, ny, half_tiles, slots = dims
+    rows, width = matrix_rows.shape
+    f32, bf16 = jnp.float32, jnp.bfloat16
+    dma = pltpu.SemaphoreType.DMA
+    hbm = pl.BlockSpec(memory_space=pltpu.HBM)
+    return pl.pallas_call(
+        functools.partial(plane_kernel, dims),
+        out_shape=jax.ShapeDtypeStruct((slots, 2 * rows, 2 * rows), f32),
+        in_specs=[hbm, hbm, hbm],
+        out_specs=pl.BlockSpec(memory_space=pltpu.VMEM),
+        scratch_shapes=[
+            pltpu.VMEM((8, 2, rows, width), f32),
+            pltpu.VMEM((rows, width), f32),
+            pltpu.VMEM((8, 2, 2, rows, width), bf16),
+            pltpu.VMEM((2, rows, width), bf16),
+            pltpu.VMEM((4, 2, 2, 2, rows, rows), f32),
+            pltpu.VMEM((2, 2 * rows, 2 * rows), f32),
+            pltpu.SMEM(tile_owner.shape, jnp.int32),
+            pltpu.SMEM(tile_slot.shape, jnp.int32),
+            pltpu.SMEM((slots + 2,), jnp.int32),
+            dma((3,)), dma((64,)), dma((64,)),
+        ],
+        compiler_params=pltpu.CompilerParams(
+            collective_id=0, has_side_effects=True,
+            vmem_limit_bytes=44 * 1024 * 1024,
+        ),
+    )(matrix_rows, tile_owner, tile_slot)
+
+
 def copy_out(in_ref, out_ref, sem):
     copy = pltpu.make_async_copy(in_ref, out_ref, sem)
     copy.start()
     copy.wait()
 
 
-def per_device(mesh_shape, matrix_rows, tile_owner, tile_slot):
+def ring_call(mesh_shape, matrix_rows, tile_owner, tile_slot):
     nx, ny = mesh_shape
     rows, width = matrix_rows.shape
     half_tiles, half_x = ny // 2, nx // 2
@@ -362,7 +687,7 @@
     reach = max(ny // 4, 1)
     f32, bf16 = jnp.float32, jnp.bfloat16
     dma = pltpu.SemaphoreType.DMA
-    packed = pl.pallas_call(
+    return pl.pallas_call(
         functools.partial(kernel, (nx, ny, half_tiles, half_x, capacity, slots)),
         out_shape=jax.ShapeDtypeStruct((slots, 2 * rows, 2 * rows), f32),
         in_specs=[
@@ -390,6 +715,15 @@
             collective_id=0, has_side_effects=True, vmem_limit_bytes=44 * 1024 * 1024
         ),
     )(matrix_rows, tile_owner, tile_slot)
+
+
+def per_device(mesh_shape, matrix_rows, tile_owner, tile_slot):
+    nx, ny = mesh_shape
+    if ny // 2 == 4 and nx == 4:
+        slots = -(-tile_owner.shape[0] // (nx * ny))
+        packed = plane_call((nx, ny, ny // 2, slots), matrix_rows, tile_owner, tile_slot)
+    else:
+        packed = ring_call(mesh_shape, matrix_rows, tile_owner, tile_slot)
     return pl.pallas_call(
         copy_out,
         out_shape=jax.ShapeDtypeStruct(packed.shape, packed.dtype),

time: 57.4 us -> 50.8 us (0.89)
  Pallas kernels: 54.8 us -> 48.2 us
    pallas_call x1, Pallas kernels: 53.7 us -> 47.1 us  [plane_call(): pl.pallas_call(functools.partial(plane_kernel, dims), out_shape=jax.Shape...]
where the time goes in v2:
time: 50.8 us; the launch traced here: 50.6 us
  Pallas kernels  48.2 us (95%)
  local copies, waits for them, and re-layouts  2.4 us (5%)
    pallas_call x1, Pallas kernels, plane_call(): pl.pallas_call(functools.partial(plane_kernel, dims), out_shape=jax.Shape...  47.1 us
    unnamed x6, local copies, waits for them, and re-layouts  2.4 us
    pallas_call x1, Pallas kernels, per_device(): pl.pallas_call(copy_out, out_shape=jax.ShapeDtypeStruct(packed.shape, pac...  1.07 us

profile of v2, /device:TPU:1, one launch (start us, length us, event | category | flops | bytes accessed | tf_op | source)
XLA Modules:
  0.0 50.6 jit_solution(8042867370081927371)
XLA Ops:
  0.0 0.0 copy-start
  0.0 1.0 %copy-done = f32[128,1024]{1,0:T(8,128)S(1)} copy-done((f32[128,1024]{1,0:T(8,128)S(1)}, f32[128,1024]{1,0:T(8,128)}, u32[]{:S(2)}) %copy-start) | copy-done | bytes 524312
  1.0 0.0 copy-start.1
  1.0 0.7 %copy-done.1 = s32[136]{0:T(256)S(1)} copy-done((s32[136]{0:T(256)S(1)}, s32[136]{0:T(256)}, u32[]{:S(2)}) %copy-start.1) | copy-done | bytes 568
  1.7 0.0 copy-start.2
  1.7 0.7 %copy-done.2 = s32[136]{0:T(256)S(1)} copy-done((s32[136]{0:T(256)S(1)}, s32[136]{0:T(256)}, u32[]{:S(2)}) %copy-start.2) | copy-done | bytes 568
  2.4 47.1 %shard_map.37.in_ref = f32[5,256,256]{2,1,0:T(8,128)S(1)} custom-call(f32[128,1024]{1,0:T(8,128)S(1)} %copy-done, s32[136]{0:T(256)S(1)} %copy-done.1, s32[136]{0:T(256)S(1)} %copy-done.2), custom_call_target="tpu_custom_call" | custom-call | tf_op jit(solution)/shard_map/pallas_call | solution.py:650
  49.5 1.1 %shard_map.38 = f32[5,256,256]{2,1,0:T(8,128)} custom-call(f32[5,256,256]{2,1,0:T(8,128)S(1)} %shard_map.37.in_ref), custom_call_target="tpu_custom_call" | custom-call | tf_op jit(solution)/shard_map/pallas_call | solution.py:727
Async XLA Ops:
  0.0 1.0 %copy-start = (f32[128,1024]{1,0:T(8,128)S(1)}, f32[128,1024]{1,0:T(8,128)}, u32[]{:S(2)}) copy-start(f32[128,1024]{1,0:T(8,128)} %rows_hbm.1) | copy-start | bytes 1572868
  1.0 0.7 %copy-start.1 = (s32[136]{0:T(256)S(1)}, s32[136]{0:T(256)}, u32[]{:S(2)}) copy-start(s32[136]{0:T(256)} %owner_hbm.1) | copy-start | bytes 1636
  1.7 0.7 %copy-start.2 = (s32[136]{0:T(256)S(1)}, s32[136]{0:T(256)}, u32[]{:S(2)}) copy-start(s32[136]{0:T(256)} %slot_hbm.1) | copy-start | bytes 1636

commit v3 on v2

--- a/solution.py
+++ b/solution.py
@@ -641,8 +641,9 @@
         copy.wait_send()
 
 
-def plane_call(dims, matrix_rows, tile_owner, tile_slot):
+def plane_call(dims, *arrays):
     nx, ny, half_tiles, slots = dims
+    matrix_rows, tile_owner, tile_slot = arrays
     rows, width = matrix_rows.shape
     f32, bf16 = jnp.float32, jnp.bfloat16
     dma = pltpu.SemaphoreType.DMA
@@ -668,7 +669,7 @@
             collective_id=0, has_side_effects=True,
             vmem_limit_bytes=44 * 1024 * 1024,
         ),
-    )(matrix_rows, tile_owner, tile_slot)
+    )(*(pltpu.with_memory_space_constraint(a, pltpu.HBM) for a in arrays))
 
 
 def copy_out(in_ref, out_ref, sem):

time: 50.8 us -> 48.3 us (0.951)
  local copies, waits for them, and re-layouts: 2.4 us -> 0 us
    unnamed x6 -> x0, local copies, waits for them, and re-layouts: 2.4 us -> none
where the time goes in v3:
time: 48.3 us; the launch traced here: 48.1 us
  Pallas kernels  48.1 us (100%)
    pallas_call x1, Pallas kernels, plane_call(): pl.pallas_call(functools.partial(plane_kernel, dims), out_shape=jax.Shape...  47.1 us
    pallas_call x1, Pallas kernels, per_device(): pl.pallas_call(copy_out, out_shape=jax.ShapeDtypeStruct(packed.shape, pac...  1.07 us

profile of v3, /device:TPU:1, one launch (start us, length us, event | category | flops | bytes accessed | tf_op | source)
XLA Modules:
  0.0 48.1 jit_solution(10745475179975245918)
XLA Ops:
  0.0 47.1 %shard_map.37.in_ref = f32[5,256,256]{2,1,0:T(8,128)S(1)} custom-call(f32[128,1024]{1,0:T(8,128)} %rows_hbm.1, s32[136]{0:T(256)} %owner_hbm.1, s32[136]{0:T(256)} %slot_hbm.1), custom_call_target="tpu_custom_call" | custom-call | tf_op jit(solution)/shard_map/pallas_call | solution.py:651
  47.1 1.1 %shard_map.38 = f32[5,256,256]{2,1,0:T(8,128)} custom-call(f32[5,256,256]{2,1,0:T(8,128)S(1)} %shard_map.37.in_ref), custom_call_target="tpu_custom_call" | custom-call | tf_op jit(solution)/shard_map/pallas_call | solution.py:728

commit v4 on v3

--- a/solution.py
+++ b/solution.py
@@ -349,11 +349,12 @@
 def plane_kernel(
     dims, rows_hbm, owner_hbm, slot_hbm, out_ref,
     gath, zfar, parts, far_parts, far, extra, owner_ref, slot_ref, todo,
-    ins, ss, rs,
+    ins, ss, rs, entered,
 ):
     nx, ny, half_tiles, slots = dims
     rows, width = zfar.shape
     half = rows // 2
+    cuts = (0, width // 2, width * 7 // 8, width)
     x = lax.axis_index("gx")
     y = lax.axis_index("gy")
     core = lax.rem(y, 2)
@@ -364,10 +365,19 @@
     across = (x, y + 2 - 4 * lax.rem(chip, 2))
     along = (x, lax.rem(y + 4, ny))
 
+    odd, high, ends = lax.rem(chip, 2), lax.div(chip, 2), jnp.where(x == nx - 1, 1, 0)
+    earlier = (core, odd, high, jnp.where(x > 0, 1, 0))
+    later = (1 - core, 1 - odd, 1 - high, 1 - ends)
     barrier = pltpu.get_barrier_semaphore()
-    peers = (sibling, across, along, right, left)
-    for other in peers:
-        pl.semaphore_signal(barrier, inc=1, device_id=other, device_id_type=MESH)
+
+    def signal_if(flag, semaphore, target):
+        @pl.when(flag == 1)
+        def _():
+            pl.semaphore_signal(semaphore, inc=1, device_id=target, device_id_type=MESH)
+
+    for flag, target in zip(later, (sibling, across, along, right)):
+        signal_if(flag, barrier, target)
+    signal_if(jnp.where(x == 0, 1, 0), barrier, left)
     loads = [
         pltpu.make_async_copy(rows_hbm, gath.at[0, core], ins.at[0]),
         pltpu.make_async_copy(owner_hbm, owner_ref, ins.at[1]),
@@ -375,7 +385,14 @@
     ]
     for copy in loads:
         copy.start()
-    pl.semaphore_wait(barrier, len(peers))
+    expected = sum(earlier) + ends
+
+    @pl.when(expected > 0)
+    def _():
+        pl.semaphore_wait(barrier, expected)
+
+    for n, target in enumerate((sibling, across, along, left)):
+        signal_if(earlier[n], entered.at[n], target)
     loads[0].wait()
 
     started, numbers = [], {}
@@ -383,14 +400,17 @@
     def number(name):
         return numbers.setdefault(name, len(numbers))
 
-    def send(name, src, dst, target):
+    def ready(name, src, dst, target):
         i = number(name)
         copy = pltpu.make_async_remote_copy(
             src_ref=src, dst_ref=dst, send_sem=ss.at[i], recv_sem=rs.at[i],
             device_id=target, device_id_type=MESH,
         )
-        copy.start()
         started.append(copy)
+        return copy
+
+    def send(*args):
+        ready(*args).start()
 
     def got(name, dst):
         i = number(name)
@@ -405,26 +425,49 @@
     def cross(where, h):
         send(("cross", where, h), block(where, core, h), block(where, core, h), sibling)
 
+    def strip(where, side, c):
+        return gath.at[where, side, :, pl.ds(cuts[c], cuts[c + 1] - cuts[c])]
+
     def crossed(where, h):
         got(("cross", where, h), block(where, twin, h))
         split(where, twin, h)
 
-    def split(where, side, h):
-        value = gath[where, side, h * half:(h + 1) * half]
+    def split_at(where, side, part):
+        value = gath[where, side, part[0], part[1]]
         hi = value.astype(jnp.bfloat16)
-        parts[where, 0, side, h * half:(h + 1) * half] = hi
-        parts[where, 1, side, h * half:(h + 1) * half] = (
+        parts[where, 0, side, part[0], part[1]] = hi
+        parts[where, 1, side, part[0], part[1]] = (
             value - hi.astype(jnp.float32)
         ).astype(jnp.bfloat16)
 
-    for h in (0, 1):
-        send(("z", 0, h), block(0, core, h), block(4, core, h), right)
-        send(("x", 0, h), block(0, core, h), block(1, core, h), across)
-        send(("y", 0, 1 - h), block(0, core, 1 - h), block(2, core, 1 - h), along)
-    for h in (0, 1):
-        cross(0, h)
+    def split(where, side, h):
+        split_at(where, side, (slice(h * half, (h + 1) * half), slice(None)))
+
+    def split_strip(side, c):
+        split_at(7, side, (slice(None), slice(cuts[c], cuts[c + 1])))
+
+    first = [
+        [ready(("cross", 0, h), block(0, core, h), block(0, core, h), sibling) for h in (0, 1)],
+        [ready(("x", 0, h), block(0, core, h), block(1, core, h), across) for h in (0, 1)],
+        [ready(("y", 0, h), block(0, core, h), block(2, core, h), along) for h in (1, 0)],
+        [ready(("z", 0, h), block(0, core, h), block(4, core, h), right) for h in (0, 1)],
+    ]
+
+    def open_way(n, early):
+        @pl.when(later[n] == (0 if early else 1))
+        def _():
+            if not early:
+                pl.semaphore_wait(entered.at[n], 1)
+            for copy in first[n]:
+                copy.start()
+
+    for n in (3, 1, 2, 0):
+        open_way(n, True)
+    for n in (1, 2, 0):
+        open_way(n, False)
     for h in (0, 1):
         split(0, core, h)
+    open_way(3, False)
     for copy in loads[1:]:
         copy.wait()
 
@@ -476,17 +519,17 @@
         preferred_element_type=jnp.float32,
     )
 
-    def product(code):
-        first, second = lax.rem(code, 8), lax.rem(lax.div(code, 8), 8)
-        both = one(
-            parts[first].reshape(4 * rows, width), parts[second, 0].reshape(2 * rows, width)
-        )
+    def product(code, lo, hi):
+        lhs, rhs = lax.rem(code, 8), lax.rem(lax.div(code, 8), 8)
+        deep = hi - lo
+
+        def part(n):
+            return parts[rhs, n, :, :, lo:hi].reshape(2 * rows, deep)
+
+        both = one(parts[lhs, :, :, :, lo:hi].reshape(4 * rows, deep), part(0))
         return both[:2 * rows] + (
             both[2 * rows:]
-            + one(
-                parts[first, 0].reshape(2 * rows, width),
-                parts[second, 1].reshape(2 * rows, width),
-            )
+            + one(parts[lhs, 0, :, :, lo:hi].reshape(2 * rows, deep), part(1))
         )
 
     got(("x", 0, 0), block(1, core, 0))
@@ -514,7 +557,7 @@
     send(("z", 1, 1), block(4, core, 1), zfar.at[pl.ds(half, half)], right)
     for h in (0, 1):
         send(("x", 4, h), block(4, core, h), block(5, core, h), across)
-        send(("y", 4, h), block(4, core, h), block(6, core, h), along)
+        send(("y", 4, 1 - h), block(4, core, 1 - h), block(6, core, 1 - h), along)
     cross(4, 1)
     split(1, core, 1)
     split(2, core, 0)
@@ -526,12 +569,26 @@
     cross(3, 0)
     got(("x", 3, 1), block(3, core, 1))
     cross(3, 1)
-    for h in (0, 1):
-        send(("z", 3, h), block(3, core, h), block(7, core, h), right)
+    for c in (0, 1):
+        send(("z", 3, c), strip(3, core, c), strip(7, core, c), right)
     split(3, core, 0)
     split(3, core, 1)
     crossed(3, 0)
     crossed(3, 1)
+
+    def corner(where, side, h):
+        return gath.at[where, side, pl.ds(h * half, half), pl.ds(cuts[2], width - cuts[2])]
+
+    got(("x", 4, 0), block(5, core, 0))
+    send(("y", 7), corner(5, core, 0), corner(7, core, 0), along)
+    got(("y", 4, 1), block(6, core, 1))
+    send(("x", 7), corner(6, core, 1), corner(7, core, 1), across)
+    cross(5, 0)
+    cross(6, 1)
+    split(5, core, 0)
+    split(6, core, 1)
+    crossed(5, 0)
+    crossed(6, 1)
 
     def split_far(h):
         part = slice(h * half, (h + 1) * half)
@@ -569,15 +626,18 @@
     for t in (0, 1):
         far_cross(0, t)
 
-    for h in (0, 1):
-        got(("x", 4, h), block(5, core, h))
-        cross(5, h)
-        got(("y", 4, h), block(6, core, h))
-        cross(6, h)
-        split(5, core, h)
-        split(6, core, h)
-        crossed(5, h)
-        crossed(6, h)
+    got(("x", 4, 1), block(5, core, 1))
+    cross(5, 1)
+    got(("y", 4, 0), block(6, core, 0))
+    cross(6, 0)
+    split(5, core, 1)
+    split(6, core, 0)
+    got(("y", 7), corner(7, core, 0))
+    got(("x", 7), corner(7, core, 1))
+    send(("cross", 7, 2), strip(7, core, 2), strip(7, core, 2), sibling)
+    split_strip(core, 2)
+    crossed(5, 1)
+    crossed(6, 0)
 
     above = jnp.where(
         lax.broadcasted_iota(jnp.int32, (2 * rows, 2 * rows), 0)
@@ -587,8 +647,17 @@
     def local(s, carry):
         code = todo[s]
         masked = jnp.where(code >= 256, 1, 0)
-        out_ref[s] = jnp.where(above * masked == 1, 0.0, product(code))
+        out_ref[s] = jnp.where(above * masked == 1, 0.0, product(code, 0, width))
         return carry
+
+    def take_strip(c):
+        got(("z", 3, c), strip(7, core, c))
+        send(("cross", 7, c), strip(7, core, c), strip(7, core, c), sibling)
+        split_strip(core, c)
+
+    def twin_strip(c):
+        got(("cross", 7, c), strip(7, twin, c))
+        split_strip(twin, c)
 
     middle = slots // 2
     lax.fori_loop(0, middle, local, 0)
@@ -598,25 +667,28 @@
     send(("fx", 3, 1), far_at(2, core, 1), far_at(3, core, 1), across)
     far_cross(1, 0)
     far_cross(2, 1)
-    got(("z", 3, 0), block(7, core, 0))
-    cross(7, 0)
+    take_strip(0)
     lax.fori_loop(middle, slots, local, 0)
-    split(7, core, 0)
-    crossed(7, 0)
+    twin_strip(2)
+    twin_strip(0)
+
+    def behind(k, carry):
+        extra[k] = product(todo[slots + k], 0, cuts[1])
+        return carry
+
+    lax.fori_loop(0, 2, behind, 0)
     got(("fx", 0, 1), far_at(1, core, 1))
     far_cross(1, 1)
     got(("fy", 0, 0), far_at(2, core, 0))
     far_cross(2, 0)
-    got(("z", 3, 1), block(7, core, 1))
-    cross(7, 1)
-    split(7, core, 1)
-    crossed(7, 1)
-
-    def behind(k, carry):
-        extra[k] = product(todo[slots + k])
+    take_strip(1)
+    twin_strip(1)
+
+    def behind_more(k, carry):
+        extra[k] = extra[k] + product(todo[slots + k], cuts[1], width)
         return carry
 
-    lax.fori_loop(0, 2, behind, 0)
+    lax.fori_loop(0, 2, behind_more, 0)
     got(("fy", 3, 0), far_at(3, core, 0))
     far_cross(3, 0)
     got(("fx", 3, 1), far_at(3, core, 1))
@@ -663,7 +735,7 @@
             pltpu.SMEM(tile_owner.shape, jnp.int32),
             pltpu.SMEM(tile_slot.shape, jnp.int32),
             pltpu.SMEM((slots + 2,), jnp.int32),
-            dma((3,)), dma((64,)), dma((64,)),
+            dma((3,)), dma((64,)), dma((64,)), pltpu.SemaphoreType.REGULAR((4,)),
         ],
         compiler_params=pltpu.CompilerParams(
             collective_id=0, has_side_effects=True,

time: 48.3 us -> 46 us (0.952)
  Pallas kernels: 48.1 us -> 45.5 us
    pallas_call x1, Pallas kernels: 47.1 us -> 44.5 us  [plane_call(): pl.pallas_call(functools.partial(plane_kernel, dims), out_shape=jax.Shape...]
where the time goes in v4:
time: 46 us; the launch traced here: 45.5 us
  Pallas kernels  45.5 us (99%)
    pallas_call x1, Pallas kernels, plane_call(): pl.pallas_call(functools.partial(plane_kernel, dims), out_shape=jax.Shape...  44.5 us
    pallas_call x1, Pallas kernels, per_device(): pl.pallas_call(copy_out, out_shape=jax.ShapeDtypeStruct(packed.shape, pac...  1.07 us

profile of v4, /device:TPU:1, one launch (start us, length us, event | category | flops | bytes accessed | tf_op | source)
XLA Modules:
  0.0 45.5 jit_solution(18066758780962476425)
XLA Ops:
  0.0 44.5 %shard_map.37.in_ref = f32[5,256,256]{2,1,0:T(8,128)S(1)} custom-call(f32[128,1024]{1,0:T(8,128)} %rows_hbm.1, s32[136]{0:T(256)} %owner_hbm.1, s32[136]{0:T(256)} %slot_hbm.1), custom_call_target="tpu_custom_call" | custom-call | tf_op jit(solution)/shard_map/pallas_call | solution.py:723
  44.5 1.1 %shard_map.38 = f32[5,256,256]{2,1,0:T(8,128)} custom-call(f32[5,256,256]{2,1,0:T(8,128)S(1)} %shard_map.37.in_ref), custom_call_target="tpu_custom_call" | custom-call | tf_op jit(solution)/shard_map/pallas_call | solution.py:800

commit v5 on v4

--- a/solution.py
+++ b/solution.py
@@ -354,7 +354,7 @@
     nx, ny, half_tiles, slots = dims
     rows, width = zfar.shape
     half = rows // 2
-    cuts = (0, width // 2, width * 7 // 8, width)
+    cuts = (0, width // 2, width)
     x = lax.axis_index("gx")
     y = lax.axis_index("gy")
     core = lax.rem(y, 2)
@@ -379,9 +379,14 @@
         signal_if(flag, barrier, target)
     signal_if(jnp.where(x == 0, 1, 0), barrier, left)
     loads = [
-        pltpu.make_async_copy(rows_hbm, gath.at[0, core], ins.at[0]),
-        pltpu.make_async_copy(owner_hbm, owner_ref, ins.at[1]),
-        pltpu.make_async_copy(slot_hbm, slot_ref, ins.at[2]),
+        pltpu.make_async_copy(
+            rows_hbm.at[pl.ds(h * half, half)], gath.at[0, core, pl.ds(h * half, half)],
+            ins.at[h],
+        )
+        for h in (0, 1)
+    ] + [
+        pltpu.make_async_copy(owner_hbm, owner_ref, ins.at[2]),
+        pltpu.make_async_copy(slot_hbm, slot_ref, ins.at[3]),
     ]
     for copy in loads:
         copy.start()
@@ -394,19 +399,26 @@
     for n, target in enumerate((sibling, across, along, left)):
         signal_if(earlier[n], entered.at[n], target)
     loads[0].wait()
-
-    started, numbers = [], {}
+    loads[1].wait()
+
+    numbers, flying, issued = {}, {}, {}
+    ways = {"x": (across, 0), "y": (along, 4), "z": (right, 8), "c": (sibling, 12)}
 
     def number(name):
         return numbers.setdefault(name, len(numbers))
 
-    def ready(name, src, dst, target):
-        i = number(name)
+    def ready(way, name, src, dst):
+        target, base = ways[way]
+        turn = issued.get(way, 0)
+        issued[way] = turn + 1
+        i, j = number(name), base + turn % 4
+        if j in flying:
+            flying[j].wait_send()
         copy = pltpu.make_async_remote_copy(
-            src_ref=src, dst_ref=dst, send_sem=ss.at[i], recv_sem=rs.at[i],
+            src_ref=src, dst_ref=dst, send_sem=ss.at[j], recv_sem=rs.at[i],
             device_id=target, device_id_type=MESH,
         )
-        started.append(copy)
+        flying[j] = copy
         return copy
 
     def send(*args):
@@ -422,15 +434,20 @@
     def block(where, side, h):
         return gath.at[where, side, pl.ds(h * half, half)]
 
-    def cross(where, h):
-        send(("cross", where, h), block(where, core, h), block(where, core, h), sibling)
+    def cross(where, h, name):
+        send("c", ("cross", name), block(where, core, h), block(where, core, h))
+
+    def crossed(where, h, name):
+        got(("cross", name), block(where, twin, h))
+        split(where, twin, h)
+
+    def both_crossed(where):
+        got(("cross", where), gath.at[where, twin])
+        split(where, twin, 0)
+        split(where, twin, 1)
 
     def strip(where, side, c):
         return gath.at[where, side, :, pl.ds(cuts[c], cuts[c + 1] - cuts[c])]
-
-    def crossed(where, h):
-        got(("cross", where, h), block(where, twin, h))
-        split(where, twin, h)
 
     def split_at(where, side, part):
         value = gath[where, side, part[0], part[1]]
@@ -447,10 +464,10 @@
         split_at(7, side, (slice(None), slice(cuts[c], cuts[c + 1])))
 
     first = [
-        [ready(("cross", 0, h), block(0, core, h), block(0, core, h), sibling) for h in (0, 1)],
-        [ready(("x", 0, h), block(0, core, h), block(1, core, h), across) for h in (0, 1)],
-        [ready(("y", 0, h), block(0, core, h), block(2, core, h), along) for h in (1, 0)],
-        [ready(("z", 0, h), block(0, core, h), block(4, core, h), right) for h in (0, 1)],
+        [ready("c", ("cross", 0), block(0, core, h), block(0, core, h)) for h in (0, 1)],
+        [ready("x", ("x", 0, h), block(0, core, h), block(1, core, h)) for h in (0, 1)],
+        [ready("y", ("y", 0, h), block(0, core, h), block(2, core, h)) for h in (1, 0)],
+        [ready("z", ("z", 0, h), block(0, core, h), block(4, core, h)) for h in (0, 1)],
     ]
 
     def open_way(n, early):
@@ -468,7 +485,7 @@
     for h in (0, 1):
         split(0, core, h)
     open_way(3, False)
-    for copy in loads[1:]:
+    for copy in loads[2:]:
         copy.wait()
 
     me = x * ny + y
@@ -532,63 +549,67 @@
             + one(parts[lhs, 0, :, :, lo:hi].reshape(2 * rows, deep), part(1))
         )
 
+    def to_zfar(h):
+        send("z", ("z", 1), block(4, core, h), zfar.at[pl.ds(h * half, half)])
+
     got(("x", 0, 0), block(1, core, 0))
-    send(("y", 3, 0), block(1, core, 0), block(3, core, 0), along)
+    send("y", ("near", 3), block(1, core, 0), block(3, core, 0))
     got(("y", 0, 1), block(2, core, 1))
-    send(("x", 3, 1), block(2, core, 1), block(3, core, 1), across)
-    cross(1, 0)
-    cross(2, 1)
+    send("x", ("near", 3), block(2, core, 1), block(3, core, 1))
+    cross(1, 0, (1, 0))
+    cross(2, 1, (2, 1))
     got(("z", 0, 0), block(4, core, 0))
-    send(("z", 1, 0), block(4, core, 0), zfar.at[pl.ds(0, half)], right)
-    cross(4, 0)
+    to_zfar(0)
+    cross(4, 0, (4, 0))
     split(1, core, 0)
     split(2, core, 1)
     split(4, core, 0)
-    crossed(0, 0)
-    crossed(0, 1)
-    crossed(1, 0)
-    crossed(2, 1)
-    crossed(4, 0)
+    both_crossed(0)
+    crossed(1, 0, (1, 0))
+    crossed(2, 1, (2, 1))
+    crossed(4, 0, (4, 0))
     got(("x", 0, 1), block(1, core, 1))
-    cross(1, 1)
+    cross(1, 1, (1, 1))
     got(("y", 0, 0), block(2, core, 0))
-    cross(2, 0)
+    cross(2, 0, (2, 0))
     got(("z", 0, 1), block(4, core, 1))
-    send(("z", 1, 1), block(4, core, 1), zfar.at[pl.ds(half, half)], right)
+    to_zfar(1)
     for h in (0, 1):
-        send(("x", 4, h), block(4, core, h), block(5, core, h), across)
-        send(("y", 4, 1 - h), block(4, core, 1 - h), block(6, core, 1 - h), along)
-    cross(4, 1)
+        send("x", ("next", h), block(4, core, h), block(5, core, h))
+        send("y", ("next", h), block(4, core, h), block(6, core, h))
+    cross(4, 1, (4, 1))
     split(1, core, 1)
     split(2, core, 0)
     split(4, core, 1)
-    crossed(1, 1)
-    crossed(2, 0)
-    crossed(4, 1)
-    got(("y", 3, 0), block(3, core, 0))
-    cross(3, 0)
-    got(("x", 3, 1), block(3, core, 1))
-    cross(3, 1)
+    crossed(1, 1, (1, 1))
+    crossed(2, 0, (2, 0))
+    crossed(4, 1, (4, 1))
+    got(("near", 3), gath.at[3, core])
     for c in (0, 1):
-        send(("z", 3, c), strip(3, core, c), strip(7, core, c), right)
+        send("z", ("z", 3, c), strip(3, core, c), strip(7, core, c))
+    for h in (0, 1):
+        cross(3, h, 3)
     split(3, core, 0)
     split(3, core, 1)
-    crossed(3, 0)
-    crossed(3, 1)
-
-    def corner(where, side, h):
-        return gath.at[where, side, pl.ds(h * half, half), pl.ds(cuts[2], width - cuts[2])]
-
-    got(("x", 4, 0), block(5, core, 0))
-    send(("y", 7), corner(5, core, 0), corner(7, core, 0), along)
-    got(("y", 4, 1), block(6, core, 1))
-    send(("x", 7), corner(6, core, 1), corner(7, core, 1), across)
-    cross(5, 0)
-    cross(6, 1)
-    split(5, core, 0)
-    split(6, core, 1)
-    crossed(5, 0)
-    crossed(6, 1)
+    both_crossed(3)
+
+    def pair(side, h):
+        return gath.at[pl.ds(5, 2), side, pl.ds(h * half, half)]
+
+    def take_next(h):
+        got(("next", h), pair(core, h))
+        cross(5, h, ("next", h))
+        cross(6, h, ("next", h))
+        split(5, core, h)
+        split(6, core, h)
+
+    def twin_next(h):
+        got(("cross", ("next", h)), pair(twin, h))
+        split(5, twin, h)
+        split(6, twin, h)
+
+    take_next(0)
+    twin_next(0)
 
     def split_far(h):
         part = slice(h * half, (h + 1) * half)
@@ -597,10 +618,15 @@
         far_parts[0, part] = hi
         far_parts[1, part] = (value - hi.astype(jnp.float32)).astype(jnp.bfloat16)
 
+    def far_at(where, side, t):
+        return far.at[where, side, t]
+
+    def far_cross(where, t):
+        send("c", ("far",), far_at(where, core, t), far_at(where, core, t))
+
     flag = jnp.where(x >= nx // 2, 1, 0)
-    got(("z", 1, 0), zfar.at[pl.ds(0, half)])
+    got(("z", 1), zfar)
     split_far(0)
-    got(("z", 1, 1), zfar.at[pl.ds(half, half)])
     split_far(1)
     for t in (0, 1):
         col = flag + 2 * lax.rem(t + lax.div(chip, 2), 2)
@@ -613,31 +639,16 @@
         for k in (0, 1):
             piece_k = full[:, k * rows:(k + 1) * rows]
             far[0, core, t, k] = jnp.where(flag == 0, piece_k, piece_k.T)
-
-    def far_at(where, side, t):
-        return far.at[where, side, t]
-
-    def far_cross(where, t):
-        send(("fcross", where, t), far_at(where, core, t), far_at(where, core, t), sibling)
-
-    for t in (0, 1):
-        send(("fx", 0, t), far_at(0, core, t), far_at(1, core, t), across)
-        send(("fy", 0, 1 - t), far_at(0, core, 1 - t), far_at(2, core, 1 - t), along)
+        if t == 0:
+            send("x", ("fx", 0), far_at(0, core, 0), far_at(1, core, 0))
+    send("y", ("fy", 1), far_at(0, core, 1), far_at(2, core, 1))
+    send("x", ("fx", 1), far_at(0, core, 1), far_at(1, core, 1))
+    send("y", ("fy", 0), far_at(0, core, 0), far_at(2, core, 0))
     for t in (0, 1):
         far_cross(0, t)
 
-    got(("x", 4, 1), block(5, core, 1))
-    cross(5, 1)
-    got(("y", 4, 0), block(6, core, 0))
-    cross(6, 0)
-    split(5, core, 1)
-    split(6, core, 0)
-    got(("y", 7), corner(7, core, 0))
-    got(("x", 7), corner(7, core, 1))
-    send(("cross", 7, 2), strip(7, core, 2), strip(7, core, 2), sibling)
-    split_strip(core, 2)
-    crossed(5, 1)
-    crossed(6, 0)
+    take_next(1)
+    twin_next(1)
 
     above = jnp.where(
         lax.broadcasted_iota(jnp.int32, (2 * rows, 2 * rows), 0)
@@ -652,50 +663,44 @@
 
     def take_strip(c):
         got(("z", 3, c), strip(7, core, c))
-        send(("cross", 7, c), strip(7, core, c), strip(7, core, c), sibling)
+        send("c", ("cross", (7, c)), strip(7, core, c), strip(7, core, c))
         split_strip(core, c)
 
     def twin_strip(c):
-        got(("cross", 7, c), strip(7, twin, c))
+        got(("cross", (7, c)), strip(7, twin, c))
         split_strip(twin, c)
+
+    def behind(k, carry):
+        extra[k] = product(todo[slots + k], 0, cuts[1])
+        return carry
+
+    def behind_more(k, carry):
+        extra[k] = extra[k] + product(todo[slots + k], cuts[1], width)
+        return carry
 
     middle = slots // 2
     lax.fori_loop(0, middle, local, 0)
-    got(("fx", 0, 0), far_at(1, core, 0))
-    send(("fy", 3, 0), far_at(1, core, 0), far_at(3, core, 0), along)
-    got(("fy", 0, 1), far_at(2, core, 1))
-    send(("fx", 3, 1), far_at(2, core, 1), far_at(3, core, 1), across)
+    got(("fx", 0), far_at(1, core, 0))
+    send("y", ("far", 3), far_at(1, core, 0), far_at(3, core, 0))
+    got(("fy", 1), far_at(2, core, 1))
+    send("x", ("far", 3), far_at(2, core, 1), far_at(3, core, 1))
     far_cross(1, 0)
     far_cross(2, 1)
     take_strip(0)
     lax.fori_loop(middle, slots, local, 0)
-    twin_strip(2)
     twin_strip(0)
-
-    def behind(k, carry):
-        extra[k] = product(todo[slots + k], 0, cuts[1])
-        return carry
-
     lax.fori_loop(0, 2, behind, 0)
-    got(("fx", 0, 1), far_at(1, core, 1))
+    got(("fx", 1), far_at(1, core, 1))
     far_cross(1, 1)
-    got(("fy", 0, 0), far_at(2, core, 0))
+    got(("fy", 0), far_at(2, core, 0))
     far_cross(2, 0)
     take_strip(1)
+    got(("far", 3), far.at[3, core])
+    far_cross(3, 0)
+    far_cross(3, 1)
     twin_strip(1)
-
-    def behind_more(k, carry):
-        extra[k] = extra[k] + product(todo[slots + k], cuts[1], width)
-        return carry
-
     lax.fori_loop(0, 2, behind_more, 0)
-    got(("fy", 3, 0), far_at(3, core, 0))
-    far_cross(3, 0)
-    got(("fx", 3, 1), far_at(3, core, 1))
-    far_cross(3, 1)
-    for where in range(4):
-        for t in (0, 1):
-            got(("fcross", where, t), far_at(where, twin, t))
+    got(("far",), far.at[:, twin])
 
     for s in range(slots):
         kind, code = kinds[s], jnp.maximum(codes[s], 0)
@@ -709,7 +714,7 @@
                 value = jnp.where(kind == 1, extra[rank, at[1], at[2]], out_ref[at])
                 value = jnp.where(kind == 2, far[where, side, t, k], value)
                 out_ref[at] = jnp.where(kind == 3, 0.0, value)
-    for copy in started:
+    for copy in flying.values():
         copy.wait_send()
 
 
@@ -735,7 +740,7 @@
             pltpu.SMEM(tile_owner.shape, jnp.int32),
             pltpu.SMEM(tile_slot.shape, jnp.int32),
             pltpu.SMEM((slots + 2,), jnp.int32),
-            dma((3,)), dma((64,)), dma((64,)), pltpu.SemaphoreType.REGULAR((4,)),
+            dma((4,)), dma((16,)), dma((30,)), pltpu.SemaphoreType.REGULAR((4,)),
         ],
         compiler_params=pltpu.CompilerParams(
             collective_id=0, has_side_effects=True,

time: 46 us -> 45.3 us (0.985)
  no operation moved by 1% of the time
where the time goes in v5:
time: 45.3 us; the launch traced here: 45.1 us
  Pallas kernels  45.1 us (100%)
    pallas_call x1, Pallas kernels, plane_call(): pl.pallas_call(functools.partial(plane_kernel, dims), out_shape=jax.Shape...  44.1 us
    pallas_call x1, Pallas kernels, per_device(): pl.pallas_call(copy_out, out_shape=jax.ShapeDtypeStruct(packed.shape, pac...  1.07 us

profile of v5, /device:TPU:1, one launch (start us, length us, event | category | flops | bytes accessed | tf_op | source)
XLA Modules:
  0.0 45.1 jit_solution(6059507450118997028)
XLA Ops:
  0.0 44.1 %shard_map.37.in_ref = f32[5,256,256]{2,1,0:T(8,128)S(1)} custom-call(f32[128,1024]{1,0:T(8,128)} %rows_hbm.1, s32[136]{0:T(256)} %owner_hbm.1, s32[136]{0:T(256)} %slot_hbm.1), custom_call_target="tpu_custom_call" | custom-call | tf_op jit(solution)/shard_map/pallas_call | solution.py:728
  44.1 1.1 %shard_map.38 = f32[5,256,256]{2,1,0:T(8,128)} custom-call(f32[5,256,256]{2,1,0:T(8,128)S(1)} %shard_map.37.in_ref), custom_call_target="tpu_custom_call" | custom-call | tf_op jit(solution)/shard_map/pallas_call | solution.py:805

commit v6 on v5

--- a/solution.py
+++ b/solution.py
@@ -366,8 +366,8 @@
     along = (x, lax.rem(y + 4, ny))
 
     odd, high, ends = lax.rem(chip, 2), lax.div(chip, 2), jnp.where(x == nx - 1, 1, 0)
-    earlier = (core, odd, high, jnp.where(x > 0, 1, 0))
-    later = (1 - core, 1 - odd, 1 - high, 1 - ends)
+    earlier = (1 - core, odd, high, jnp.where(x > 0, 1, 0))
+    later = (core, 1 - odd, 1 - high, 1 - ends)
     barrier = pltpu.get_barrier_semaphore()
 
     def signal_if(flag, semaphore, target):
@@ -398,8 +398,6 @@
 
     for n, target in enumerate((sibling, across, along, left)):
         signal_if(earlier[n], entered.at[n], target)
-    loads[0].wait()
-    loads[1].wait()
 
     numbers, flying, issued = {}, {}, {}
     ways = {"x": (across, 0), "y": (along, 4), "z": (right, 8), "c": (sibling, 12)}
@@ -407,7 +405,7 @@
     def number(name):
         return numbers.setdefault(name, len(numbers))
 
-    def ready(way, name, src, dst):
+    def ready(way, name, src, dst, other=None):
         target, base = ways[way]
         turn = issued.get(way, 0)
         issued[way] = turn + 1
@@ -419,7 +417,12 @@
             device_id=target, device_id_type=MESH,
         )
         flying[j] = copy
-        return copy
+        if other is None:
+            return copy
+        return copy, pltpu.make_async_remote_copy(
+            src_ref=other, dst_ref=dst, send_sem=ss.at[j], recv_sem=rs.at[i],
+            device_id=target, device_id_type=MESH,
+        )
 
     def send(*args):
         ready(*args).start()
@@ -463,11 +466,11 @@
     def split_strip(side, c):
         split_at(7, side, (slice(None), slice(cuts[c], cuts[c + 1])))
 
+    own = [rows_hbm.at[pl.ds(h * half, half)] for h in (0, 1)]
     first = [
-        [ready("c", ("cross", 0), block(0, core, h), block(0, core, h)) for h in (0, 1)],
-        [ready("x", ("x", 0, h), block(0, core, h), block(1, core, h)) for h in (0, 1)],
-        [ready("y", ("y", 0, h), block(0, core, h), block(2, core, h)) for h in (1, 0)],
-        [ready("z", ("z", 0, h), block(0, core, h), block(4, core, h)) for h in (0, 1)],
+        [ready("x", ("x", 0, h), block(0, core, h), block(1, core, h), own[h]) for h in (0, 1)],
+        [ready("y", ("y", 0, h), block(0, core, h), block(2, core, h), own[h]) for h in (1, 0)],
+        [ready("z", ("z", 0, h), block(0, core, h), block(4, core, h), own[h]) for h in (0, 1)],
     ]
 
     def open_way(n, early):
@@ -475,13 +478,22 @@
         def _():
             if not early:
                 pl.semaphore_wait(entered.at[n], 1)
-            for copy in first[n]:
-                copy.start()
-
-    for n in (3, 1, 2, 0):
+            for copies in first[n - 1]:
+                copies[1 if early else 0].start()
+
+    for n in (1, 2, 3):
         open_way(n, True)
-    for n in (1, 2, 0):
+    loads[0].wait()
+    loads[1].wait()
+    for n in (1, 2):
         open_way(n, False)
+
+    @pl.when(later[0] == 1)
+    def _():
+        pl.semaphore_wait(entered.at[0], 1)
+
+    for h in (0, 1):
+        cross(0, h, 0)
     for h in (0, 1):
         split(0, core, h)
     open_way(3, False)

time: 45.3 us -> 45 us (level)
  no operation moved by 1% of the time
where the time goes in v6:
time: 45 us; the launch traced here: 44.9 us
  Pallas kernels  44.8 us (100%)
    pallas_call x1, Pallas kernels, plane_call(): pl.pallas_call(functools.partial(plane_kernel, dims), out_shape=jax.Shape...  43.8 us
    pallas_call x1, Pallas kernels, per_device(): pl.pallas_call(copy_out, out_shape=jax.ShapeDtypeStruct(packed.shape, pac...  1.07 us

profile of v6, /device:TPU:1, one launch (start us, length us, event | category | flops | bytes accessed | tf_op | source)
XLA Modules:
  0.0 44.9 jit_solution(17601396636651843529)
XLA Ops:
  0.0 43.8 %shard_map.37.in_ref = f32[5,256,256]{2,1,0:T(8,128)S(1)} custom-call(f32[128,1024]{1,0:T(8,128)} %rows_hbm.1, s32[136]{0:T(256)} %owner_hbm.1, s32[136]{0:T(256)} %slot_hbm.1), custom_call_target="tpu_custom_call" | custom-call | tf_op jit(solution)/shard_map/pallas_call | solution.py:740
  43.8 1.1 %shard_map.38 = f32[5,256,256]{2,1,0:T(8,128)} custom-call(f32[5,256,256]{2,1,0:T(8,128)S(1)} %shard_map.37.in_ref), custom_call_target="tpu_custom_call" | custom-call | tf_op jit(solution)/shard_map/pallas_call | solution.py:817

commit v7 on v6

--- a/solution.py
+++ b/solution.py
@@ -400,7 +400,7 @@
         signal_if(earlier[n], entered.at[n], target)
 
     numbers, flying, issued = {}, {}, {}
-    ways = {"x": (across, 0), "y": (along, 4), "z": (right, 8), "c": (sibling, 12)}
+    ways = {"x": (across, 0), "y": (along, 5), "z": (right, 10), "c": (sibling, 15)}
 
     def number(name):
         return numbers.setdefault(name, len(numbers))
@@ -409,7 +409,7 @@
         target, base = ways[way]
         turn = issued.get(way, 0)
         issued[way] = turn + 1
-        i, j = number(name), base + turn % 4
+        i, j = number(name), base + turn % 5
         if j in flying:
             flying[j].wait_send()
         copy = pltpu.make_async_remote_copy(
@@ -562,7 +562,7 @@
         )
 
     def to_zfar(h):
-        send("z", ("z", 1), block(4, core, h), zfar.at[pl.ds(h * half, half)])
+        send("z", ("z", 1, h), block(4, core, h), zfar.at[pl.ds(h * half, half)])
 
     got(("x", 0, 0), block(1, core, 0))
     send("y", ("near", 3), block(1, core, 0), block(3, core, 0))
@@ -637,25 +637,69 @@
         send("c", ("far",), far_at(where, core, t), far_at(where, core, t))
 
     flag = jnp.where(x >= nx // 2, 1, 0)
-    got(("z", 1), zfar)
-    split_far(0)
-    split_far(1)
-    for t in (0, 1):
+    def far_tile(t, lo, hi):
+        count = hi - lo
         col = flag + 2 * lax.rem(t + lax.div(chip, 2), 2)
         both = one(
-            far_parts[...].reshape(2 * rows, width), parts[col, 0].reshape(2 * rows, width)
-        )
-        full = both[:rows] + (
-            both[rows:] + one(far_parts[0], parts[col, 1].reshape(2 * rows, width))
-        )
+            far_parts[:, lo:hi].reshape(2 * count, width),
+            parts[col, 0].reshape(2 * rows, width),
+        )
+        return both[:count] + (
+            both[count:] + one(far_parts[0, lo:hi], parts[col, 1].reshape(2 * rows, width))
+        )
+
+    def far_rows(t, h):
+        full = far_tile(t, h * half, (h + 1) * half)
         for k in (0, 1):
-            piece_k = full[:, k * rows:(k + 1) * rows]
-            far[0, core, t, k] = jnp.where(flag == 0, piece_k, piece_k.T)
-        if t == 0:
-            send("x", ("fx", 0), far_at(0, core, 0), far_at(1, core, 0))
-    send("y", ("fy", 1), far_at(0, core, 1), far_at(2, core, 1))
-    send("x", ("fx", 1), far_at(0, core, 1), far_at(1, core, 1))
-    send("y", ("fy", 0), far_at(0, core, 0), far_at(2, core, 0))
+            far[0, core, t, k, h * half:(h + 1) * half] = full[:, k * rows:(k + 1) * rows]
+
+    def far_turned(t):
+        full = far_tile(t, 0, rows)
+        for k in (0, 1):
+            far[0, core, t, k] = full[:, k * rows:(k + 1) * rows].T
+
+    def far_piece(where, t, h):
+        return far.at[where, core, t, :, pl.ds(h * half, half)]
+
+    def far_ready(h):
+        return [
+            ready("x", ("fx", 0, h), far_piece(0, 0, h), far_piece(1, 0, h)),
+            ready("y", ("fy", 1, h), far_piece(0, 1, h), far_piece(2, 1, h)),
+            ready("x", ("fx", 1), far_piece(0, 1, h), far_piece(1, 1, h)),
+            ready("y", ("fy", 0), far_piece(0, 0, h), far_piece(2, 0, h)),
+        ]
+
+    got(("z", 1, 0), zfar.at[pl.ds(0, half)])
+    split_far(0)
+    upper = far_ready(0)
+
+    @pl.when(flag == 0)
+    def _():
+        far_rows(0, 0)
+        far_rows(1, 0)
+        for copy in upper:
+            copy.start()
+
+    got(("z", 1, 1), zfar.at[pl.ds(half, half)])
+    split_far(1)
+    lower = far_ready(1)
+
+    @pl.when(flag == 0)
+    def _():
+        far_rows(0, 1)
+        lower[0].start()
+        far_rows(1, 1)
+        for copy in lower[1:]:
+            copy.start()
+
+    @pl.when(flag == 1)
+    def _():
+        far_turned(0)
+        far_turned(1)
+        for pair_of in zip(upper, lower):
+            for copy in pair_of:
+                copy.start()
+
     for t in (0, 1):
         far_cross(0, t)
 
@@ -692,10 +736,11 @@
 
     middle = slots // 2
     lax.fori_loop(0, middle, local, 0)
-    got(("fx", 0), far_at(1, core, 0))
-    send("y", ("far", 3), far_at(1, core, 0), far_at(3, core, 0))
-    got(("fy", 1), far_at(2, core, 1))
-    send("x", ("far", 3), far_at(2, core, 1), far_at(3, core, 1))
+    for h in (0, 1):
+        got(("fx", 0, h), far_piece(1, 0, h))
+        send("y", ("far", 3), far_piece(1, 0, h), far_piece(3, 0, h))
+        got(("fy", 1, h), far_piece(2, 1, h))
+        send("x", ("far", 3), far_piece(2, 1, h), far_piece(3, 1, h))
     far_cross(1, 0)
     far_cross(2, 1)
     take_strip(0)
@@ -752,7 +797,7 @@
             pltpu.SMEM(tile_owner.shape, jnp.int32),
             pltpu.SMEM(tile_slot.shape, jnp.int32),
             pltpu.SMEM((slots + 2,), jnp.int32),
-            dma((4,)), dma((16,)), dma((30,)), pltpu.SemaphoreType.REGULAR((4,)),
+            dma((4,)), dma((20,)), dma((33,)), pltpu.SemaphoreType.REGULAR((4,)),
         ],
         compiler_params=pltpu.CompilerParams(
             collective_id=0, has_side_effects=True,

time: 45 us -> 44.1 us (0.980)
  Pallas kernels: 44.8 us -> 43.9 us
    pallas_call x1, Pallas kernels: 43.8 us -> 42.9 us  [plane_call(): pl.pallas_call(functools.partial(plane_kernel, dims), out_shape=jax.Shape...]
where the time goes in v7:
time: 44.1 us; the launch traced here: 43.9 us
  Pallas kernels  43.9 us (100%)
    pallas_call x1, Pallas kernels, plane_call(): pl.pallas_call(functools.partial(plane_kernel, dims), out_shape=jax.Shape...  42.9 us
    pallas_call x1, Pallas kernels, per_device(): pl.pallas_call(copy_out, out_shape=jax.ShapeDtypeStruct(packed.shape, pac...  1.07 us

profile of v7, /device:TPU:1, one launch (start us, length us, event | category | flops | bytes accessed | tf_op | source)
XLA Modules:
  0.0 43.9 jit_solution(2927160086536773923)
XLA Ops:
  0.0 42.9 %shard_map.37.in_ref = f32[5,256,256]{2,1,0:T(8,128)S(1)} custom-call(f32[128,1024]{1,0:T(8,128)} %rows_hbm.1, s32[136]{0:T(256)} %owner_hbm.1, s32[136]{0:T(256)} %slot_hbm.1), custom_call_target="tpu_custom_call" | custom-call | tf_op jit(solution)/shard_map/pallas_call | solution.py:785
  42.9 1.1 %shard_map.38 = f32[5,256,256]{2,1,0:T(8,128)} custom-call(f32[5,256,256]{2,1,0:T(8,128)S(1)} %shard_map.37.in_ref), custom_call_target="tpu_custom_call" | custom-call | tf_op jit(solution)/shard_map/pallas_call | solution.py:862

commit v8 on v7

--- a/solution.py
+++ b/solution.py
@@ -379,14 +379,9 @@
         signal_if(flag, barrier, target)
     signal_if(jnp.where(x == 0, 1, 0), barrier, left)
     loads = [
-        pltpu.make_async_copy(
-            rows_hbm.at[pl.ds(h * half, half)], gath.at[0, core, pl.ds(h * half, half)],
-            ins.at[h],
-        )
-        for h in (0, 1)
-    ] + [
-        pltpu.make_async_copy(owner_hbm, owner_ref, ins.at[2]),
-        pltpu.make_async_copy(slot_hbm, slot_ref, ins.at[3]),
+        pltpu.make_async_copy(rows_hbm, gath.at[0, core], ins.at[0]),
+        pltpu.make_async_copy(owner_hbm, owner_ref, ins.at[1]),
+        pltpu.make_async_copy(slot_hbm, slot_ref, ins.at[2]),
     ]
     for copy in loads:
         copy.start()
@@ -400,16 +395,16 @@
         signal_if(earlier[n], entered.at[n], target)
 
     numbers, flying, issued = {}, {}, {}
-    ways = {"x": (across, 0), "y": (along, 5), "z": (right, 10), "c": (sibling, 15)}
+    ways = {"x": (across, 0, 5), "y": (along, 5, 5), "z": (right, 10, 3), "c": (sibling, 13, 4)}
 
     def number(name):
         return numbers.setdefault(name, len(numbers))
 
     def ready(way, name, src, dst, other=None):
-        target, base = ways[way]
+        target, base, pool = ways[way]
         turn = issued.get(way, 0)
         issued[way] = turn + 1
-        i, j = number(name), base + turn % 5
+        i, j = number(name), base + turn % pool
         if j in flying:
             flying[j].wait_send()
         copy = pltpu.make_async_remote_copy(
@@ -484,7 +479,6 @@
     for n in (1, 2, 3):
         open_way(n, True)
     loads[0].wait()
-    loads[1].wait()
     for n in (1, 2):
         open_way(n, False)
 
@@ -497,7 +491,7 @@
     for h in (0, 1):
         split(0, core, h)
     open_way(3, False)
-    for copy in loads[2:]:
+    for copy in loads[1:]:
         copy.wait()
 
     me = x * ny + y
@@ -665,8 +659,8 @@
         return [
             ready("x", ("fx", 0, h), far_piece(0, 0, h), far_piece(1, 0, h)),
             ready("y", ("fy", 1, h), far_piece(0, 1, h), far_piece(2, 1, h)),
-            ready("x", ("fx", 1), far_piece(0, 1, h), far_piece(1, 1, h)),
-            ready("y", ("fy", 0), far_piece(0, 0, h), far_piece(2, 0, h)),
+            ready("x", ("f2",), far_piece(0, 1, h), far_piece(1, 1, h)),
+            ready("y", ("f2",), far_piece(0, 0, h), far_piece(2, 0, h)),
         ]
 
     got(("z", 1, 0), zfar.at[pl.ds(0, half)])
@@ -738,23 +732,23 @@
     lax.fori_loop(0, middle, local, 0)
     for h in (0, 1):
         got(("fx", 0, h), far_piece(1, 0, h))
-        send("y", ("far", 3), far_piece(1, 0, h), far_piece(3, 0, h))
+        send("y", ("far", 3, h), far_piece(1, 0, h), far_piece(3, 0, h))
         got(("fy", 1, h), far_piece(2, 1, h))
-        send("x", ("far", 3), far_piece(2, 1, h), far_piece(3, 1, h))
+        send("x", ("far", 3, h), far_piece(2, 1, h), far_piece(3, 1, h))
     far_cross(1, 0)
     far_cross(2, 1)
     take_strip(0)
     lax.fori_loop(middle, slots, local, 0)
     twin_strip(0)
     lax.fori_loop(0, 2, behind, 0)
-    got(("fx", 1), far_at(1, core, 1))
+    got(("f2",), far.at[1, core])
     far_cross(1, 1)
-    got(("fy", 0), far_at(2, core, 0))
     far_cross(2, 0)
     take_strip(1)
-    got(("far", 3), far.at[3, core])
-    far_cross(3, 0)
-    far_cross(3, 1)
+    for h in (0, 1):
+        both_tiles = far.at[3, core, :, :, pl.ds(h * half, half)]
+        got(("far", 3, h), both_tiles)
+        send("c", ("far",), both_tiles, both_tiles)
     twin_strip(1)
     lax.fori_loop(0, 2, behind_more, 0)
     got(("far",), far.at[:, twin])
@@ -797,7 +791,7 @@
             pltpu.SMEM(tile_owner.shape, jnp.int32),
             pltpu.SMEM(tile_slot.shape, jnp.int32),
             pltpu.SMEM((slots + 2,), jnp.int32),
-            dma((4,)), dma((20,)), dma((33,)), pltpu.SemaphoreType.REGULAR((4,)),
+            dma((3,)), dma((17,)), dma((33,)), pltpu.SemaphoreType.REGULAR((4,)),
         ],
         compiler_params=pltpu.CompilerParams(
             collective_id=0, has_side_effects=True,

time: 44.1 us -> 44 us (level)
  no operation moved by 1% of the time
where the time goes in v8:
time: 44 us; the launch traced here: 43.7 us
  Pallas kernels  43.7 us (99%)
    pallas_call x1, Pallas kernels, plane_call(): pl.pallas_call(functools.partial(plane_kernel, dims), out_shape=jax.Shape...  42.6 us
    pallas_call x1, Pallas kernels, per_device(): pl.pallas_call(copy_out, out_shape=jax.ShapeDtypeStruct(packed.shape, pac...  1.07 us

profile of v8, /device:TPU:1, one launch (start us, length us, event | category | flops | bytes accessed | tf_op | source)
XLA Modules:
  0.0 43.7 jit_solution(6384686144928617037)
XLA Ops:
  0.0 42.6 %shard_map.37.in_ref = f32[5,256,256]{2,1,0:T(8,128)S(1)} custom-call(f32[128,1024]{1,0:T(8,128)} %rows_hbm.1, s32[136]{0:T(256)} %owner_hbm.1, s32[136]{0:T(256)} %slot_hbm.1), custom_call_target="tpu_custom_call" | custom-call | tf_op jit(solution)/shard_map/pallas_call | solution.py:779
  42.6 1.1 %shard_map.38 = f32[5,256,256]{2,1,0:T(8,128)} custom-call(f32[5,256,256]{2,1,0:T(8,128)S(1)} %shard_map.37.in_ref), custom_call_target="tpu_custom_call" | custom-call | tf_op jit(solution)/shard_map/pallas_call | solution.py:856

commit v9 on v8

--- a/solution.py
+++ b/solution.py
@@ -354,7 +354,7 @@
     nx, ny, half_tiles, slots = dims
     rows, width = zfar.shape
     half = rows // 2
-    cuts = (0, width // 2, width)
+    cuts = (0, width * 5 // 8, width)
     x = lax.axis_index("gx")
     y = lax.axis_index("gy")
     core = lax.rem(y, 2)
@@ -800,12 +800,6 @@
     )(*(pltpu.with_memory_space_constraint(a, pltpu.HBM) for a in arrays))
 
 
-def copy_out(in_ref, out_ref, sem):
-    copy = pltpu.make_async_copy(in_ref, out_ref, sem)
-    copy.start()
-    copy.wait()
-
-
 def ring_call(mesh_shape, matrix_rows, tile_owner, tile_slot):
     nx, ny = mesh_shape
     rows, width = matrix_rows.shape
@@ -853,14 +847,7 @@
         packed = plane_call((nx, ny, ny // 2, slots), matrix_rows, tile_owner, tile_slot)
     else:
         packed = ring_call(mesh_shape, matrix_rows, tile_owner, tile_slot)
-    return pl.pallas_call(
-        copy_out,
-        out_shape=jax.ShapeDtypeStruct(packed.shape, packed.dtype),
-        in_specs=[pl.BlockSpec(memory_space=pltpu.VMEM)],
-        out_specs=pl.BlockSpec(memory_space=pl.ANY),
-        scratch_shapes=[pltpu.SemaphoreType.DMA(())],
-        compiler_params=pltpu.CompilerParams(vmem_limit_bytes=4 * 1024 * 1024),
-    )(packed)
+    return packed
 
 
 def solution(mesh):

time: 44 us -> 44 us (level)
  Pallas kernels: 43.7 us -> 42.6 us
  local copies, waits for them, and re-layouts: 0 us -> 1.06 us
    pallas_call x1 -> x0, Pallas kernels: 1.07 us -> none  [per_device(): pl.pallas_call(copy_out, out_shape=jax.ShapeDtypeStruct(packed.shape, pac...]
    unnamed x0 -> x1, local copies, waits for them, and re-layouts: none -> 1.06 us
where the time goes in v9:
time: 44 us; the launch traced here: 43.7 us
  Pallas kernels  42.6 us (97%)
  local copies, waits for them, and re-layouts  1.06 us (2%)
    pallas_call x1, Pallas kernels, plane_call(): pl.pallas_call(functools.partial(plane_kernel, dims), out_shape=jax.Shape...  42.6 us
    unnamed x1, local copies, waits for them, and re-layouts  1.06 us

profile of v9, /device:TPU:1, one launch (start us, length us, event | category | flops | bytes accessed | tf_op | source)
XLA Modules:
  0.0 43.7 jit_solution(15124887361967963476)
XLA Ops:
  0.0 42.6 %shard_map.37 = f32[5,256,256]{2,1,0:T(8,128)S(1)} custom-call(f32[128,1024]{1,0:T(8,128)} %rows_hbm.1, s32[136]{0:T(256)} %owner_hbm.1, s32[136]{0:T(256)} %slot_hbm.1), custom_call_target="tpu_custom_call" | custom-call | tf_op jit(solution)/shard_map/pallas_call | solution.py:779
  42.6 1.1 %copy.5 = f32[5,256,256]{2,1,0:T(8,128)} copy(f32[5,256,256]{2,1,0:T(8,128)S(1)} %shard_map.37) | data formatting | bytes 2621440

commit v10 on v9

--- a/solution.py
+++ b/solution.py
@@ -365,19 +365,6 @@
     across = (x, y + 2 - 4 * lax.rem(chip, 2))
     along = (x, lax.rem(y + 4, ny))
 
-    odd, high, ends = lax.rem(chip, 2), lax.div(chip, 2), jnp.where(x == nx - 1, 1, 0)
-    earlier = (1 - core, odd, high, jnp.where(x > 0, 1, 0))
-    later = (core, 1 - odd, 1 - high, 1 - ends)
-    barrier = pltpu.get_barrier_semaphore()
-
-    def signal_if(flag, semaphore, target):
-        @pl.when(flag == 1)
-        def _():
-            pl.semaphore_signal(semaphore, inc=1, device_id=target, device_id_type=MESH)
-
-    for flag, target in zip(later, (sibling, across, along, right)):
-        signal_if(flag, barrier, target)
-    signal_if(jnp.where(x == 0, 1, 0), barrier, left)
     loads = [
         pltpu.make_async_copy(rows_hbm, gath.at[0, core], ins.at[0]),
         pltpu.make_async_copy(owner_hbm, owner_ref, ins.at[1]),
@@ -385,6 +372,19 @@
     ]
     for copy in loads:
         copy.start()
+    odd, high, ends = lax.rem(chip, 2), lax.div(chip, 2), jnp.where(x == nx - 1, 1, 0)
+    earlier = (1 - core, odd, high, jnp.where(x > 0, 1, 0))
+    later = (core, 1 - odd, 1 - high, 1 - ends)
+    barrier = pltpu.get_barrier_semaphore()
+
+    def signal_if(flag, semaphore, target):
+        @pl.when(flag == 1)
+        def _():
+            pl.semaphore_signal(semaphore, inc=1, device_id=target, device_id_type=MESH)
+
+    for flag, target in zip(later, (sibling, across, along, right)):
+        signal_if(flag, barrier, target)
+    signal_if(jnp.where(x == 0, 1, 0), barrier, left)
     expected = sum(earlier) + ends
 
     @pl.when(expected > 0)

time: 44 us -> 44 us (level)
  no operation moved by 1% of the time
where the time goes in v10:
time: 44 us; the launch traced here: 43.7 us
  Pallas kernels  42.6 us (97%)
  local copies, waits for them, and re-layouts  1.06 us (2%)
    pallas_call x1, Pallas kernels, plane_call(): pl.pallas_call(functools.partial(plane_kernel, dims), out_shape=jax.Shape...  42.6 us
    unnamed x1, local copies, waits for them, and re-layouts  1.06 us

profile of v10, /device:TPU:1, one launch (start us, length us, event | category | flops | bytes accessed | tf_op | source)
XLA Modules:
  0.0 43.7 jit_solution(11934255495908267665)
XLA Ops:
  0.0 42.6 %shard_map.37 = f32[5,256,256]{2,1,0:T(8,128)S(1)} custom-call(f32[128,1024]{1,0:T(8,128)} %rows_hbm.1, s32[136]{0:T(256)} %owner_hbm.1, s32[136]{0:T(256)} %slot_hbm.1), custom_call_target="tpu_custom_call" | custom-call | tf_op jit(solution)/shard_map/pallas_call | solution.py:779
  42.6 1.1 %copy.5 = f32[5,256,256]{2,1,0:T(8,128)} copy(f32[5,256,256]{2,1,0:T(8,128)S(1)} %shard_map.37) | data formatting | bytes 2621440
